TPU v7x, 8 devices: a whole 2x2x1 slice. The times are simulated.
8 devices in a mesh: data: 2 (over z, y), model: 4 (over x, core).
Axes of the slice: x: 2, y: 2, z: 1, core: 2. Of those that a mesh axis runs over, the one named last changes fastest.
Arguments:
- tokens: bfloat16 [16384, 2048], P('data')
- w_query: bfloat16 [2048, 2048], P('data', 'model')
- w_kv: bfloat16 [2048, 256], P('data')
- w_out: bfloat16 [2048, 2048], P('model', 'data')
- ln_gain: float32 [2048], replicated
- positions: int32 [256], replicated
- grad_out: bfloat16 [16384, 2048], P('data')
Outputs:
- output 1: bfloat16 [16384, 2048], P('data')
- output 2: bfloat16 [16384, 2048], P('data')
- output 3: bfloat16 [2048, 2048], P('data', 'model')
- output 4: bfloat16 [2048, 256], P('data')
- output 5: bfloat16 [2048, 2048], P('model', 'data')
All inputs are finite; a program needn't handle non-finite values.
Results may differ from a plain program's by a relative error of at most 0.0145341.
Values are sent between devices in bfloat16 or wider.
A program may use at most 1 GiB of HBM per device.

v0:
```python
import functools

import jax
import jax.numpy as jnp
from jax import lax
from jax.experimental import pallas as pl
from jax.experimental.pallas import tpu as pltpu
from jax.sharding import PartitionSpec as P


NORM_EPS = 1e-6
LOG2E = 1.4426950408889634
BF16, F32 = jnp.bfloat16, jnp.float32
NN = (((1,), (0,)), ((), ()))
NT = (((1,), (1,)), ((), ()))
TN = (((0,), (0,)), ((), ()))
MESH = pl.DeviceIdType.MESH
ANY = pl.BlockSpec(memory_space=pl.ANY)
VMEM = pl.BlockSpec(memory_space=pltpu.VMEM)
LIMIT = 62 * 2**20


def dot(a, b, dims):
    return lax.dot_general(a, b, dims, preferred_element_type=F32)


def place():
    d, m = lax.axis_index("data"), lax.axis_index("model")
    x, c = m // 2, m % 2
    return d, m, x, c, (1 - d, m), (d, 2 * (1 - x) + c), (d, 2 * x + (1 - c))


def entry_barrier(peers):
    barrier = pltpu.get_barrier_semaphore()
    for peer in peers:
        pl.semaphore_signal(barrier, inc=1, device_id=peer, device_id_type=MESH)
    pl.semaphore_wait(barrier, len(peers))


def remote(src, dst, send, recv, peer):
    return pltpu.make_async_remote_copy(src_ref=src, dst_ref=dst, send_sem=send, recv_sem=recv, device_id=peer, device_id_type=MESH)


class Gather:
    def __init__(self, piece, full, region, send, recv, local):
        self.piece, self.full, self.region = piece, full, region
        self.send, self.recv, self.local = send, recv, local

    def copies(self):
        d, m, x, c, yn, xn, pn = place()
        ym, xm = (1 - d, m), (d, 2 * (1 - x) + c)
        full, reg, s, r = self.full, self.region, self.send, self.recv
        at = lambda dm, part=None: full.at[reg(dm[0], dm[1], part)]
        diag = (1 - d, 2 * (1 - x) + c)
        own = at((d, m))
        first = [remote(self.piece, own, s.at[0], r.at[0], yn), remote(self.piece, own, s.at[1], r.at[1], xn), remote(self.piece, own, s.at[2], r.at[2], pn)]
        second = [
            remote(at(ym, 0), at(ym, 0), s.at[3], r.at[3], xn),
            remote(at(xm, 1), at(xm, 1), s.at[4], r.at[4], yn),
            remote(at(ym), at(ym), s.at[5], r.at[5], pn),
            remote(at(xm), at(xm), s.at[6], r.at[6], pn),
        ]
        third = [remote(at(diag, 0), at(diag, 0), s.at[7], r.at[7], pn), remote(at(diag, 1), at(diag, 1), s.at[8], r.at[8], pn)]
        mine = pltpu.make_async_copy(self.piece, own, self.local)
        return first, second, third, mine

    def start(self):
        first, _, _, mine = self.copies()
        for copy in first:
            copy.start()
        mine.start()

    def middle(self):
        first, second, _, _ = self.copies()
        first[1].wait_recv()
        second[1].start()
        second[3].start()
        first[0].wait_recv()
        second[0].start()
        second[2].start()

    def own_half(self):
        first, second, _, mine = self.copies()
        mine.wait()
        first[2].wait_recv()
        second[2].wait_recv()

    def finish(self):
        first, second, third, _ = self.copies()
        second[0].wait_recv()
        third[0].start()
        second[1].wait_recv()
        third[1].start()
        second[3].wait_recv()
        third[0].wait_recv()
        third[1].wait_recv()
        for copy in first + second + third:
            copy.wait_send()


def q_region(rows, cols, d, m, part):
    if part is None:
        return pl.ds(d * rows, rows), pl.ds(pl.multiple_of(m * cols, cols), cols)
    return pl.ds(d * rows + part * (rows // 2), rows // 2), pl.ds(pl.multiple_of(m * cols, cols), cols)


def o_region(rows, cols, d, m, part):
    if part is None:
        return pl.ds(m * rows, rows), pl.ds(pl.multiple_of(d * cols, cols), cols)
    return pl.ds(m * rows + part * (rows // 2), rows // 2), pl.ds(pl.multiple_of(d * cols, cols), cols)


def front_kernel(half, tok, wq, wkv, wo, gain, wcat, wo_full, hidden, means, inv_stds, proj, q_send, q_recv, o_send, o_recv, kv_send, kv_recv, local):
    d, _, x, c, yn, xn, pn = place()
    rows, cols = wq.shape
    depth, width = wo_full.shape[1], wo_full.shape[0]
    krows, pair = wkv.shape[0] // 2, wkv.shape[1]
    entry_barrier((yn, xn, pn))
    k_here = lambda dd, cc: wcat.at[pl.ds(dd * 2 * krows + cc * krows, krows), pl.ds(width, pair)]
    k_out = remote(wkv.at[pl.ds(c * krows, krows), :], k_here(d, c), kv_send.at[0], kv_recv.at[0], yn)
    k_fwd = remote(k_here(1 - d, c), k_here(1 - d, c), kv_send.at[1], kv_recv.at[1], pn)
    k_own = pltpu.make_async_copy(wkv, wcat.at[pl.ds(d * 2 * krows, 2 * krows), pl.ds(width, pair)], local.at[2])
    k_out.start()
    gather_q = Gather(wq, wcat, functools.partial(q_region, rows, cols), q_send, q_recv, local.at[0])
    gather_o = Gather(wo, wo_full, functools.partial(o_region, wo.shape[0], wo.shape[1]), o_send, o_recv, local.at[1])
    gather_q.start()
    k_own.start()

    def norm_block(tok_blk, hid_blk, mean_blk, inv_blk):
        rows_f = tok_blk[...].astype(F32)
        mean = jnp.mean(rows_f, axis=-1, keepdims=True)
        centred = rows_f - mean
        inv_std = lax.rsqrt(jnp.mean(centred * centred, axis=-1, keepdims=True) + NORM_EPS)
        hid_blk[...] = (centred * inv_std * gain[...]).astype(BF16)
        mean_blk[...] = jnp.broadcast_to(mean, mean_blk.shape)
        inv_blk[...] = jnp.broadcast_to(inv_std, inv_blk.shape)

    tile = 512
    pltpu.emit_pipeline(
        norm_block,
        grid=(half // tile,),
        in_specs=[pl.BlockSpec((tile, depth), lambda i: (i, 0))],
        out_specs=[pl.BlockSpec((tile, depth), lambda i: (i, 0))] + [pl.BlockSpec((tile, 128), lambda i: (i, 0))] * 2,
    )(tok.at[pl.ds(c * half, half), :], hidden, means, inv_stds)

    big = 1024

    def block(a, b, out):
        out[...] = dot(a[...], b[...], NN).astype(BF16)

    def run(col, cols_n, row_block, row_blocks):
        span = pl.ds(pl.multiple_of(col, cols_n), cols_n)
        pltpu.emit_pipeline(
            block,
            grid=(row_blocks,),
            in_specs=[pl.BlockSpec((big, depth), lambda i: (row_block + i, 0)), pl.BlockSpec((depth, cols_n), lambda i: (0, 0))],
            out_specs=[pl.BlockSpec((big, cols_n), lambda i: (row_block + i, 0))],
        )(hidden, wcat.at[:, span], proj.at[:, span])

    blocks = half // big
    k_out.wait_recv()
    k_fwd.start()
    k_own.wait()
    k_fwd.wait_recv()
    run(width, pair, 0, blocks)
    gather_q.middle()
    gather_o.start()
    gather_q.own_half()
    run(x * (width // 2), width // 2, 0, blocks)
    gather_q.finish()
    run((1 - x) * (width // 2), width // 2, 0, blocks // 2)
    gather_o.middle()
    run((1 - x) * (width // 2), width // 2, blocks // 2, blocks - blocks // 2)
    gather_o.own_half()
    gather_o.finish()
    k_out.wait_send()
    k_fwd.wait_send()


def mm_kernel(dims, off, a, b, out):
    out[...] = dot(a[...], b[...], dims).astype(BF16)


def matmul(a, b, dims, rows, row_block, tile=1024):
    depth = a.shape[1]
    width = b.shape[1] if dims == NN else b.shape[0]
    b_spec = pl.BlockSpec((depth, tile), lambda j, i, off: (0, j)) if dims == NN else pl.BlockSpec((tile, depth), lambda j, i, off: (j, 0))
    return pl.pallas_call(
        functools.partial(mm_kernel, dims),
        grid_spec=pltpu.PrefetchScalarGridSpec(
            num_scalar_prefetch=1,
            grid=(width // tile, rows // tile),
            in_specs=[pl.BlockSpec((tile, depth), lambda j, i, off: (off[0] + i, 0)), b_spec],
            out_specs=pl.BlockSpec((tile, tile), lambda j, i, off: (i, j)),
        ),
        out_shape=jax.ShapeDtypeStruct((rows, width), BF16),
        cost_estimate=pl.CostEstimate(flops=2 * rows * depth * width, bytes_accessed=2 * (rows * depth + depth * width + rows * width), transcendentals=0),
        compiler_params=pltpu.CompilerParams(vmem_limit_bytes=LIMIT),
    )(row_block, a, b)


def attend_kernel(heads, head_dim, qkv_ref, do_ref, pos_c_ref, pos_r_ref, o_ref, dqkv_ref, seen, pt, dst):
    seq, width = do_ref.shape
    q_ref, dq_ref = qkv_ref, dqkv_ref

    @pl.when(pl.program_id(0) == 0)
    def _():
        seen[...] = jnp.where(pos_c_ref[...] <= pos_r_ref[...], 1.0, -1.0)

    k, v = qkv_ref[:, width : width + head_dim], qkv_ref[:, width + head_dim :]
    kt, vt = k.T, v.T
    scale = head_dim ** -0.5
    cols = lambda h: slice(h * head_dim, (h + 1) * head_dim)
    lanes = lambda h: slice(h * seq, (h + 1) * seq)
    scores, grads, total = {}, {}, [None, None]

    def scored(h):
        scores[h] = dot(k, q_ref[:, cols(h)], NT)
        grads[h] = dot(v, do_ref[:, cols(h)], NT)

    def softmax(h):
        s = jnp.where(seen[...] > 0, scores.pop(h) * (scale * LOG2E), -1e30)
        e = jnp.exp2(s - jnp.max(s, axis=0, keepdims=True))
        p = e * (1.0 / jnp.sum(e, axis=0, keepdims=True))
        pt[:, lanes(h)] = p.astype(BF16)
        dp = grads.pop(h)
        dst[:, lanes(h)] = (p * (dp - jnp.sum(p * dp, axis=0, keepdims=True))).astype(BF16)

    def mixed(h):
        o_ref[:, cols(h)] = dot(vt, pt[:, lanes(h)], NN).T.astype(BF16)
        dq_ref[:, cols(h)] = (dot(kt, dst[:, lanes(h)], NN).T * scale).astype(BF16)
        dv = dot(pt[:, lanes(h)], do_ref[:, cols(h)], NN)
        dk = dot(dst[:, lanes(h)], q_ref[:, cols(h)], NN)
        total[0] = dk if total[0] is None else total[0] + dk
        total[1] = dv if total[1] is None else total[1] + dv

    for t in range(heads + 2):
        if t < heads:
            scored(t)
        if 0 <= t - 2:
            mixed(t - 2)
        if 0 <= t - 1 < heads:
            softmax(t - 1)
    dqkv_ref[:, width : width + head_dim] = (total[0] * scale).astype(BF16)
    dqkv_ref[:, width + head_dim :] = total[1].astype(BF16)


def attend(proj, grad_mixed, positions):
    rows, width = grad_mixed.shape
    seq, total = positions.shape[0], proj.shape[1]
    head_dim = (total - width) // 2
    heads = width // head_dim
    wide = pl.BlockSpec((seq, width), lambda i: (i, 0))
    wider = pl.BlockSpec((seq, total), lambda i: (i, 0))
    return pl.pallas_call(
        functools.partial(attend_kernel, heads, head_dim),
        grid=(rows // seq,),
        in_specs=[wider, wide, pl.BlockSpec((seq, 1), lambda i: (0, 0)), pl.BlockSpec((1, seq), lambda i: (0, 0))],
        out_specs=[wide, wider],
        out_shape=[jax.ShapeDtypeStruct((rows, width), BF16), jax.ShapeDtypeStruct((rows, total), BF16)],
        scratch_shapes=[pltpu.VMEM((seq, seq), F32), pltpu.VMEM((seq, heads * seq), BF16), pltpu.VMEM((seq, heads * seq), BF16)],
        cost_estimate=pl.CostEstimate(flops=12 * rows * seq * width, bytes_accessed=8 * rows * width, transcendentals=rows * seq * heads),
        compiler_params=pltpu.CompilerParams(vmem_limit_bytes=LIMIT),
    )(proj, grad_mixed, positions.reshape(seq, 1), positions.reshape(1, seq))


def give_kernel(off, a, b, out):
    part = dot(a[...], b[...], TN)

    @pl.when(pl.program_id(2) == 0)
    def _():
        out[...] = part

    @pl.when(pl.program_id(2) > 0)
    def _():
        out[...] += part


def keep_kernel(axis, off, a, b, got, send, keep):
    part = dot(a[...], b[...], TN)
    k = pl.program_id(2)

    def add(out):
        @pl.when(k == 0)
        def _():
            out[...] = got[...] + part

        @pl.when(k > 0)
        def _():
            out[...] += part

    pl.when(pl.program_id(axis) == 0)(lambda: add(send))
    pl.when(pl.program_id(axis) == 1)(lambda: add(keep))


def wgrad(a, b, offs, shape, tiles, got=None, axis=None):
    bm, bn, deep = tiles
    height, width = shape
    grid = (height // bm, width // bn, a.shape[0] // deep)
    half = lambda t, ax, off: jnp.where(t == 0, 1 - off[3], off[3]) if axis == ax else t
    in_specs = [
        pl.BlockSpec((deep, bm), lambda i, j, k, off: (k, off[0] + half(i, 0, off))),
        pl.BlockSpec((deep, bn), lambda i, j, k, off: (off[1] + k, off[2] + half(j, 1, off))),
    ]
    cost = pl.CostEstimate(flops=2 * a.shape[0] * height * width, bytes_accessed=2 * a.shape[0] * (height + width), transcendentals=0)
    params = pltpu.CompilerParams(vmem_limit_bytes=LIMIT)
    if got is None:
        return pl.pallas_call(
            give_kernel,
            grid_spec=pltpu.PrefetchScalarGridSpec(
                num_scalar_prefetch=1, grid=grid, in_specs=in_specs, out_specs=pl.BlockSpec((bm, bn), lambda i, j, k, off: (i, j))
            ),
            out_shape=jax.ShapeDtypeStruct(shape, F32),
            cost_estimate=cost,
            compiler_params=params,
        )(offs, a, b)
    piece = pl.BlockSpec((bm, bn), lambda i, j, k, off: (0, 0))
    return pl.pallas_call(
        functools.partial(keep_kernel, axis),
        grid_spec=pltpu.PrefetchScalarGridSpec(
            num_scalar_prefetch=1,
            grid=grid,
            in_specs=in_specs + [pl.BlockSpec((bm, bn), lambda i, j, k, off: (half(i, 0, off), half(j, 1, off)))],
            out_specs=[piece, piece],
        ),
        out_shape=[jax.ShapeDtypeStruct((bm, bn), F32)] * 2,
        cost_estimate=cost,
        compiler_params=params,
    )(offs, a, b, got)


def out_kernel(off, a, b, full, send):
    block = dot(a[...], b[...], NN).astype(BF16)
    full[...] = block
    send[...] = block


def project_out(mixed, wo, core, tile=1024):
    rows, depth = mixed.shape
    width = wo.shape[1]
    blocks = rows // tile
    return pl.pallas_call(
        out_kernel,
        grid_spec=pltpu.PrefetchScalarGridSpec(
            num_scalar_prefetch=1,
            grid=(width // tile, blocks),
            in_specs=[pl.BlockSpec((tile, depth), lambda j, i, off: (i, 0)), pl.BlockSpec((depth, tile), lambda j, i, off: (0, j))],
            out_specs=[pl.BlockSpec((tile, tile), lambda j, i, off: (off[0] * blocks + i, j)), pl.BlockSpec((tile, tile), lambda j, i, off: (i, j))],
        ),
        out_shape=[jax.ShapeDtypeStruct((2 * rows, width), BF16), jax.ShapeDtypeStruct((rows, width), BF16)],
        cost_estimate=pl.CostEstimate(flops=2 * rows * depth * width, bytes_accessed=2 * rows * (depth + 2 * width), transcendentals=0),
        compiler_params=pltpu.CompilerParams(vmem_limit_bytes=LIMIT),
    )(core, mixed, wo)


def grad_tok_kernel(passing, off, gqkv, wcat, gain, tok, means, inv_stds, *refs):
    if passing:
        got, _, _, full, send, y_full = refs
        y_full[...] = got[...]
    else:
        full, send = refs
    mean, inv_std = means[:, :1], inv_stds[:, :1]
    g = dot(gqkv[...], wcat[...], NT) * gain[...]
    normed = (tok[...].astype(F32) - mean) * inv_std
    block = (inv_std * (g - jnp.mean(g, axis=-1, keepdims=True) - normed * jnp.mean(g * normed, axis=-1, keepdims=True))).astype(BF16)
    full[...] = block
    send[...] = block


def grad_tok(gqkv, wcat, gain, tok, means, inv_stds, core, part, earlier=None, tile=512):
    rows, total = gqkv.shape
    depth = wcat.shape[0]
    blocks = rows // tile
    steps = blocks // 2
    first = part * steps
    whole = lambda i, off: (0, 0)
    once = pl.Buffered(1)
    in_specs = [
        pl.BlockSpec((tile, total), lambda i, off: (first + i, 0)),
        pl.BlockSpec((depth, total), whole, pipeline_mode=once),
        pl.BlockSpec((1, depth), whole, pipeline_mode=once),
        pl.BlockSpec((tile, depth), lambda i, off: (off[0] * blocks + first + i, 0)),
        pl.BlockSpec((tile, 128), lambda i, off: (first + i, 0)),
        pl.BlockSpec((tile, 128), lambda i, off: (first + i, 0)),
    ]
    own = pl.BlockSpec((tile, depth), lambda i, off: (off[0] * blocks + first + i, 0))
    out_specs = [own, pl.BlockSpec((tile, depth), lambda i, off: (i, 0))]
    out_shape = [jax.ShapeDtypeStruct((2 * rows, depth), BF16), jax.ShapeDtypeStruct((rows // 2, depth), BF16)]
    args, aliases = [core, gqkv, wcat, gain, tok, means, inv_stds], {}
    if earlier is not None:
        dx, y, got = earlier
        args += [got, dx, y]
        wide = 2 * tile
        in_specs += [pl.BlockSpec((wide, depth), lambda i, off: (i, 0)), ANY, ANY]
        out_specs.append(pl.BlockSpec((wide, depth), lambda i, off: ((1 - off[0]) * steps + i, 0)))
        out_shape.append(jax.ShapeDtypeStruct(y.shape, BF16))
        aliases = {8: 0, 9: 2}
    return pl.pallas_call(
        functools.partial(grad_tok_kernel, earlier is not None),
        grid_spec=pltpu.PrefetchScalarGridSpec(num_scalar_prefetch=1, grid=(steps,), in_specs=in_specs, out_specs=out_specs),
        out_shape=out_shape,
        input_output_aliases=aliases,
        cost_estimate=pl.CostEstimate(flops=rows * depth * total, bytes_accessed=5 * rows * depth, transcendentals=0),
        compiler_params=pltpu.CompilerParams(vmem_limit_bytes=LIMIT),
    )(*args)


def fill_kernel(off, got, _, out):
    out[...] = got[...]


def fill(full, got, core, part, tile=1024):
    rows, width = got.shape
    blocks = rows // tile
    return pl.pallas_call(
        fill_kernel,
        grid_spec=pltpu.PrefetchScalarGridSpec(
            num_scalar_prefetch=1,
            grid=(blocks,),
            in_specs=[pl.BlockSpec((tile, width), lambda i, off: (i, 0)), ANY],
            out_specs=pl.BlockSpec((tile, width), lambda i, off: ((1 - off[0]) * 2 * blocks + part * blocks + i, 0)),
        ),
        out_shape=jax.ShapeDtypeStruct(full.shape, full.dtype),
        input_output_aliases={2: 0},
        cost_estimate=pl.CostEstimate(flops=rows * width, bytes_accessed=4 * rows * width, transcendentals=0),
        compiler_params=pltpu.CompilerParams(vmem_limit_bytes=LIMIT),
    )(core, got, full)


def after(value, *others):
    return lax.optimization_barrier((value,) + others)[0]


def solution(mesh):
    model_size = mesh.shape["model"]
    cores = [(i, i ^ 1) for i in range(model_size)]
    datas = [(0, 1), (1, 0)]
    sems = lambda n: pltpu.SemaphoreType.DMA((n,))

    def layer(tok, wq_blk, wkv_blk, wo_blk, ln_gain, positions, grad):
        count, depth = tok.shape
        half = count // 2
        width = wq_blk.shape[1] * model_size
        pair = wkv_blk.shape[1]
        piece = width // model_size
        m = lax.axis_index("model")
        d = lax.axis_index("data")
        x, c = m // 2, m % 2
        gain = ln_gain.reshape(1, depth)
        core = c.reshape(1).astype(jnp.int32)
        index = lambda *v: jnp.stack([jnp.asarray(t, jnp.int32) for t in v])

        def swap(a):
            return lax.ppermute(a, "model", cores)

        def cross(a):
            return lax.ppermute(a, "data", datas)


        wcat, wo, hidden, means, inv_stds, proj = pl.pallas_call(
            functools.partial(front_kernel, half),
            in_specs=[ANY, VMEM, VMEM, VMEM, VMEM],
            out_specs=[ANY] * 6,
            out_shape=[
                jax.ShapeDtypeStruct((depth, width + pair), BF16),
                jax.ShapeDtypeStruct((width, depth), BF16),
                jax.ShapeDtypeStruct((half, depth), BF16),
                jax.ShapeDtypeStruct((half, 128), F32),
                jax.ShapeDtypeStruct((half, 128), F32),
                jax.ShapeDtypeStruct((half, width + pair), BF16),
            ],
            scratch_shapes=[sems(9), sems(9), sems(9), sems(9), sems(2), sems(2), sems(3)],
            compiler_params=pltpu.CompilerParams(collective_id=0, has_side_effects=True, vmem_limit_bytes=LIMIT),
        )(tok, wq_blk, wkv_blk, wo_blk, gain)

        grad_mixed = matmul(grad, wo, NT, half, core * (half // 1024))
        mixed, gqkv = attend(proj, grad_mixed, positions)

        deep = 2048
        mine, other = 2 * x + c, 2 * x + 1 - c
        row_o = c * (half // deep)
        give_o = wgrad(mixed, grad, index(other, row_o, 0, 0), (piece, depth), (piece, depth // 2, deep))
        got_o = swap(give_o)
        give_q = wgrad(after(hidden, give_o), gqkv, index(0, 0, other, 0), (depth, piece), (depth // 2, piece, deep))
        got_q = swap(give_q)
        part_kv = wgrad(after(hidden, give_q), gqkv, index(0, 0, width // pair, 0), (depth, pair), (depth // 2, pair, deep))
        send_o, keep_o = wgrad(after(mixed, part_kv), grad, index(mine, row_o, 0, d), (piece, depth), (piece, depth // 2, deep), got_o, 1)
        data_o = cross(send_o)
        send_q, keep_q = wgrad(after(hidden, send_o), gqkv, index(0, 0, mine, d), (depth, piece), (depth // 2, piece, deep), got_q, 0)
        data_q = cross(send_q)

        def halves(a, i, axis):
            size = a.shape[axis] // 2
            return lax.dynamic_slice_in_dim(a, i * size, size, axis), lax.dynamic_slice_in_dim(a, (1 - i) * size, size, axis)

        kv_keep, kv_give = halves(part_kv, c, 1)
        kv_sum = kv_keep + swap(kv_give)
        kv_keep, kv_give = halves(kv_sum, d, 0)
        kv_data = cross(kv_give)

        y, y_send = project_out(after(mixed, send_q, kv_sum), wo, core)
        y_got = swap(y_send)
        kv_cols = (kv_keep + kv_data).astype(BF16)
        kv_other = swap(kv_cols)
        grad_w_out = (keep_o + data_o).astype(BF16)
        dx, dx_send = grad_tok(after(gqkv, y_send, grad_w_out, kv_cols), wcat, gain, tok, means, inv_stds, core, 0)
        dx_got_0 = swap(dx_send)
        grad_w_query = (keep_q + data_q).astype(BF16)
        grad_w_kv = jnp.where(c == 0, jnp.concatenate([kv_cols, kv_other], axis=1), jnp.concatenate([kv_other, kv_cols], axis=1))
        dx, dx_send, y = grad_tok(after(gqkv, dx_send, grad_w_query, grad_w_kv), wcat, gain, tok, means, inv_stds, core, 1, (dx, y, y_got))
        dx_got_1 = swap(dx_send)
        dx = fill(dx, dx_got_0, core, 0)
        dx = fill(dx, dx_got_1, core, 1)
        return y, dx, grad_w_query, grad_w_kv, grad_w_out

    return jax.shard_map(
        layer,
        mesh=mesh,
        in_specs=(P("data", None), P("data", "model"), P("data", None), P("model", "data"), P(), P(), P("data", None)),
        out_specs=(P("data", None), P("data", None), P("data", "model"), P("data", None), P("model", "data")),
        check_vma=False,
    )
```

profile of v0, /device:TPU:0, one launch (start us, length us, event | category | flops | bytes accessed | tf_op | source)
XLA Modules:
  0.0 507.8 jit_solution(9569114968934984305)
XLA Ops:
  0.7 1.5 copy.16.pos_c_ref
  2.1 100.5 %shard_map.110 = (bf16[2048,2304]{1,0:T(8,128)(2,1)}, bf16[2048,2048]{1,0:T(8,128)(2,1)}, bf16[4096,2048]{1,0:T(8,128)(2,1)}, f32[4096,128]{1,0:T(8,128)}, f32[4...) custom-call(bf16[8192,2048]{1,0:T(8,128)(2,1)} %tok.5, bf16[1024,512]{1,0:T(8,128)(2,1)} %wq.1, bf16[1024,256]{1,0:T(8,128)(2,1)} %wkv.1, ...), custom_call_target="tpu_custom_call" | custom-call | tf_op jit(solution)/shard_map/pallas_call | solution.py:460
  102.7 41.2 %shard_map.111.do_ref = bf16[4096,2048]{1,0:T(8,128)(2,1)} custom-call(s32[1]{0:T(128)S(6)} %mul.22.off, bf16[8192,2048]{1,0:T(8,128)(2,1)} %b.3, bf16[2048,2048]{1,0:T(8,128)(2,1)} %get-tuple-element.32.b), custom_call_target="tpu_custom_call" | custom-call | flops 34359738368 | bytes 41943040 | tf_op jit(solution)/shard_map/pallas_call | solution.py:188
  143.9 67.1 %shard_map.112 = (bf16[4096,2048]{1,0:T(8,128)(2,1)}, bf16[4096,2304]{1,0:T(8,128)(2,1)}) custom-call(bf16[4096,2304]{1,0:T(8,128)(2,1)} %get-tuple-element.31.qkv_ref, bf16[4096,2048]{1,0:T(8,128)(2,1)} %shard_map.111.do_ref, s32[256,1]{1,0:T(8,128)} %copy.16.pos_c_ref, s32[1,256]{1,0:T(1,128)} %bitcast.12), custom_call_target="tpu_custom_call" | custom-call | flops 25769803776 | bytes 67108864 | tf_op jit(solution)/shard_map/pallas_call | solution.py:255
  211.0 0.6 pad_add_fusion.2
  211.6 16.1 %shard_map.113 = f32[512,2048]{1,0:T(8,128)} custom-call(s32[4]{0:T(128)} %get-tuple-element.57.off, bf16[4096,2048]{1,0:T(8,128)(2,1)} %get-tuple-element.42.a, bf16[8192,2048]{1,0:T(8,128)(2,1)} %b.3), custom_call_target="tpu_custom_call" | custom-call | flops 8589934592 | bytes 20971520 | tf_op jit(solution)/shard_map/pallas_call | solution.py:308
  227.7 0.1 collective-permute-start
  227.8 16.1 %shard_map.114 = f32[2048,512]{1,0:T(8,128)} custom-call(s32[4]{0:T(128)} %get-tuple-element.58.off, bf16[4096,2048]{1,0:T(8,128)(2,1)} %get-tuple-element.40.a, bf16[4096,2304]{1,0:T(8,128)(2,1)} %get-tuple-element.51.b.gqkv), custom_call_target="tpu_custom_call" | custom-call | flops 8589934592 | bytes 20971520 | tf_op jit(solution)/shard_map/pallas_call | solution.py:308
  244.0 0.4 collective-permute-start.1
  244.4 11.7 %shard_map.115 = f32[2048,256]{1,0:T(8,128)} custom-call(s32[4]{0:T(128)} %constant.45.clone.1.off, bf16[4096,2048]{1,0:T(8,128)(2,1)} %get-tuple-element.40.a, bf16[4096,2304]{1,0:T(8,128)(2,1)} %get-tuple-element.51.b.gqkv), custom_call_target="tpu_custom_call" | custom-call | flops 4294967296 | bytes 18874368 | tf_op jit(solution)/shard_map/pallas_call | solution.py:308
  256.0 1.3 constant_dynamic-slice_fusion.1
  257.3 0.1 collective-permute-start.2
  257.5 0.6 add_add_fusion.off
  258.1 2.1 collective-permute-done.2
  260.2 1.6 dynamic-slice_add_fusion
  261.8 0.0 collective-permute-done.got
  261.8 17.7 %shard_map.116 = (f32[512,1024]{1,0:T(8,128)}, f32[512,1024]{1,0:T(8,128)}) custom-call(s32[4]{0:T(128)} %add_add_fusion.off, bf16[4096,2048]{1,0:T(8,128)(2,1)} %get-tuple-element.42.a, bf16[8192,2048]{1,0:T(8,128)(2,1)} %b.3, f32[512,2048]{1,0:T(8,128)} %collective-permute-done.got), custom_call_target="tpu_custom_call" | custom-call | flops 8589934592 | bytes 20971520 | tf_op jit(solution)/shard_map/pallas_call | solution.py:318
  279.5 0.0 collective-permute-done.1.got
  279.5 17.5 %shard_map.117 = (f32[1024,512]{1,0:T(8,128)}, f32[1024,512]{1,0:T(8,128)}) custom-call(s32[4]{0:T(128)} %get-tuple-element.59.off, bf16[4096,2048]{1,0:T(8,128)(2,1)} %get-tuple-element.40.a, bf16[4096,2304]{1,0:T(8,128)(2,1)} %get-tuple-element.51.b.gqkv, f32[2048,512]{1,0:T(8,128)} %collective-permute-done.1.got), custom_call_target="tpu_custom_call" | custom-call | flops 8589934592 | bytes 20971520 | tf_op jit(solution)/shard_map/pallas_call | solution.py:318
  297.0 42.1 %shard_map.118 = (bf16[8192,2048]{1,0:T(8,128)(2,1)}, bf16[4096,2048]{1,0:T(8,128)(2,1)}) custom-call(s32[1]{0:T(128)} %bitcast.off, bf16[4096,2048]{1,0:T(8,128)(2,1)} %get-tuple-element.42.a, bf16[2048,2048]{1,0:T(8,128)(2,1)} %get-tuple-element.32.b), custom_call_target="tpu_custom_call" | custom-call | flops 34359738368 | bytes 50331648 | tf_op jit(solution)/shard_map/pallas_call | solution.py:342
  339.1 0.1 collective-permute-start.7
  339.2 1.5 collective-permute-start.3
  340.8 0.6 collective-permute-start.4
  341.3 57.3 %collective-permute-done.4 = f32[1024,128]{1,0:T(8,128)S(1)} collective-permute-done((f32[1024,128]{1,0:T(8,128)S(1)}, f32[1024,128]{1,0:T(8,128)S(1)}, u32[]{:S(2)}, u32[]{:S(2)}) %collective-permute-start.4) | collective-permute-done | bytes 524320 | tf_op jit(solution)/shard_map/ppermute | solution.py:457
  398.6 0.1 add_convert_fusion.2
  398.6 0.0 collective-permute-start.6
  398.7 1.5 collective-permute-done.6
  400.2 1.0 maximum_select_fusion
  401.2 1.5 collective-permute-start.5
  402.7 0.0 collective-permute-done.3
  402.7 3.5 add_convert_fusion.1
  406.2 32.2 %shard_map.119 = (bf16[8192,2048]{1,0:T(8,128)(2,1)}, bf16[2048,2048]{1,0:T(8,128)(2,1)}) custom-call(s32[1]{0:T(128)} %bitcast.off, bf16[4096,2304]{1,0:T(8,128)(2,1)} %get-tuple-element.51.b.gqkv, bf16[2048,2304]{1,0:T(8,128)(2,1)} %get-tuple-element.46.wcat, f32[1,2048]{1,0:T(1,128)} %bitcast.9, bf16[8192,2048]{1,0:T(8,128)(2,1)} %tok.5, ...), custom_call_target="tpu_custom_call" | custom-call | flops 19327352832 | bytes 41943040 | tf_op jit(solution)/shard_map/pallas_call | solution.py:398
  438.3 0.0 collective-permute-start.9
  438.4 10.8 %collective-permute-done.5 = f32[1024,512]{1,0:T(8,128)} collective-permute-done((f32[1024,512]{1,0:T(8,128)}, f32[1024,512]{1,0:T(8,128)}, u32[]{:S(2)}, u32[]{:S(2)}) %collective-permute-start.5) | collective-permute-done | bytes 2097184 | tf_op jit(solution)/shard_map/ppermute | solution.py:457
  449.2 3.5 add_convert_fusion
  452.7 0.0 collective-permute-done.7.refs_0_
  452.7 35.5 %shard_map.120 = (bf16[8192,2048]{1,0:T(8,128)(2,1)}, bf16[2048,2048]{1,0:T(8,128)(2,1)}, bf16[8192,2048]{1,0:T(8,128)(2,1)}) custom-call(s32[1]{0:T(128)} %bitcast.off, bf16[4096,2304]{1,0:T(8,128)(2,1)} %get-tuple-element.51.b.gqkv, bf16[2048,2304]{1,0:T(8,128)(2,1)} %get-tuple-element.46.wcat, ...), custom_call_target="tpu_custom_call", output_to_operand_aliasing={{0}: (8, {}), {2}: (9, {})} | custom-call | flops 19327352832 | bytes 41943040 | tf_op jit(solution)/shard_map/pallas_call | solution.py:398
  488.2 0.0 collective-permute-start.8
  488.2 0.0 collective-permute-done.9.got
  488.2 5.9 %shard_map.121._ = bf16[8192,2048]{1,0:T(8,128)(2,1)} custom-call(s32[1]{0:T(128)} %bitcast.off, bf16[2048,2048]{1,0:T(8,128)(2,1)} %collective-permute-done.9.got, bf16[8192,2048]{1,0:T(8,128)(2,1)} %get-tuple-element.56._), custom_call_target="tpu_custom_call", output_to_operand_aliasing={{}: (2, {})} | custom-call | flops 4194304 | bytes 16777216 | tf_op jit(solution)/shard_map/pallas_call | solution.py:415
  494.1 7.6 %collective-permute-done.8.got = bf16[2048,2048]{1,0:T(8,128)(2,1)} collective-permute-done((bf16[2048,2048]{1,0:T(8,128)(2,1)}, bf16[2048,2048]{1,0:T(8,128)(2,1)}, u32[]{:S(2)}, u32[]{:S(2)}) %collective-permute-start.8) | collective-permute-done | bytes 8388640 | tf_op jit(solution)/shard_map/ppermute | solution.py:454
  501.7 5.9 %shard_map.122 = bf16[8192,2048]{1,0:T(8,128)(2,1)} custom-call(s32[1]{0:T(128)} %bitcast.off, bf16[2048,2048]{1,0:T(8,128)(2,1)} %collective-permute-done.8.got, bf16[8192,2048]{1,0:T(8,128)(2,1)} %shard_map.121._), custom_call_target="tpu_custom_call", output_to_operand_aliasing={{}: (2, {})} | custom-call | flops 4194304 | bytes 16777216 | tf_op jit(solution)/shard_map/pallas_call | solution.py:415
  (2 shorter events, 0.0 us)
Async XLA Ops:
  227.7 34.1 %collective-permute-start = (f32[512,2048]{1,0:T(8,128)}, f32[512,2048]{1,0:T(8,128)}, u32[]{:S(2)}, u32[]{:S(2)}) collective-permute-start(f32[512,2048]{1,0:T(8,128)} %shard_map.113), channel_id=1, source_target_pairs={{0,1},{1,0},{2,3},{3,2},{4,5},{5,4},{6,7},{7,6}} | collective-permute-start | bytes 12582920 | tf_op jit(solution)/shard_map/ppermute | solution.py:454
  244.0 35.5 %collective-permute-start.1 = (f32[2048,512]{1,0:T(8,128)}, f32[2048,512]{1,0:T(8,128)}, u32[]{:S(2)}, u32[]{:S(2)}) collective-permute-start(f32[2048,512]{1,0:T(8,128)} %shard_map.114), channel_id=1, source_target_pairs={{0,1},{1,0},{2,3},{3,2},{4,5},{5,4},{6,7},{7,6}} | collective-permute-start | bytes 12582920 | tf_op jit(solution)/shard_map/ppermute | solution.py:454
  257.3 2.8 collective-permute-start.2
  339.1 113.6 %collective-permute-start.7 = (bf16[4096,2048]{1,0:T(8,128)(2,1)}, bf16[4096,2048]{1,0:T(8,128)(2,1)}, u32[]{:S(2)}, u32[]{:S(2)}) collective-permute-start(bf16[4096,2048]{1,0:T(8,128)(2,1)} %get-tuple-element.43), channel_id=1, source_target_pairs={{0,1},{1,0},{2,3},{3,2},{4,5},{5,4},{6,7},{7,6}} | collective-permute-start | bytes 50331656 | tf_op jit(solution)/shard_map/ppermute | solution.py:454
  339.2 63.4 %collective-permute-start.3 = (f32[512,1024]{1,0:T(8,128)}, f32[512,1024]{1,0:T(8,128)}, u32[]{:S(2)}, u32[]{:S(2)}) collective-permute-start(f32[512,1024]{1,0:T(8,128)} %get-tuple-element.39), channel_id=1, source_target_pairs={{0,4},{4,0},{1,5},{5,1},{2,6},{6,2},{3,7},{7,3}} | collective-permute-start | bytes 6291464 | tf_op jit(solution)/shard_map/ppermute | solution.py:457
  340.8 57.8 %collective-permute-start.4 = (f32[1024,128]{1,0:T(8,128)S(1)}, f32[1024,128]{1,0:T(8,128)S(1)}, u32[]{:S(2)}, u32[]{:S(2)}) collective-permute-start(f32[1024,128]{1,0:T(8,128)S(1)} %constant_dynamic-slice_fusion), channel_id=1, source_target_pairs={{0,4},{4,0},{1,5},{5,1},{2,6},{6,2},{3,7},{7,3}} | collective-permute-start | bytes 1572872 | tf_op jit(solution)/shard_map/ppermute | solution.py:457
  398.6 1.6 collective-permute-start.6
  401.2 48.0 %collective-permute-start.5 = (f32[1024,512]{1,0:T(8,128)}, f32[1024,512]{1,0:T(8,128)}, u32[]{:S(2)}, u32[]{:S(2)}) collective-permute-start(f32[1024,512]{1,0:T(8,128)} %get-tuple-element.41), channel_id=1, source_target_pairs={{0,4},{4,0},{1,5},{5,1},{2,6},{6,2},{3,7},{7,3}} | collective-permute-start | bytes 6291464 | tf_op jit(solution)/shard_map/ppermute | solution.py:457
  438.3 49.9 %collective-permute-start.9 = (bf16[2048,2048]{1,0:T(8,128)(2,1)}, bf16[2048,2048]{1,0:T(8,128)(2,1)}, u32[]{:S(2)}, u32[]{:S(2)}) collective-permute-start(bf16[2048,2048]{1,0:T(8,128)(2,1)} %get-tuple-element.49), channel_id=1, source_target_pairs={{0,1},{1,0},{2,3},{3,2},{4,5},{5,4},{6,7},{7,6}} | collective-permute-start | bytes 25165832 | tf_op jit(solution)/shard_map/ppermute | solution.py:454
  488.2 13.5 %collective-permute-start.8 = (bf16[2048,2048]{1,0:T(8,128)(2,1)}, bf16[2048,2048]{1,0:T(8,128)(2,1)}, u32[]{:S(2)}, u32[]{:S(2)}) collective-permute-start(bf16[2048,2048]{1,0:T(8,128)(2,1)} %get-tuple-element.55), channel_id=1, source_target_pairs={{0,1},{1,0},{2,3},{3,2},{4,5},{5,4},{6,7},{7,6}} | collective-permute-start | bytes 25165832 | tf_op jit(solution)/shard_map/ppermute | solution.py:454
where the time goes:
time: 517 us; the launch traced here: 508 us
  Pallas kernels  409 us (79%)
  waiting for transfers between devices  79.3 us (15%)
  other arithmetic  10.9 us (2%)
    pallas_call x1, Pallas kernels, layer(): pl.pallas_call(functools.partial(front_kernel, half), in_specs=[ANY, VMEM...  101 us
    ppermute x3, waiting for transfers between devices, cross(): return lax.ppermute(a, 'data', datas)  68.1 us
    pallas_call x2, Pallas kernels, grad_tok(): pl.pallas_call(functools.partial(grad_tok_kernel, earlier is not None), g...  67.7 us
    pallas_call x1, Pallas kernels, attend(): pl.pallas_call(functools.partial(attend_kernel, heads, head_dim), grid=(r...  67.1 us
    pallas_call x3, Pallas kernels, wgrad(): pl.pallas_call(give_kernel, grid_spec=pltpu.PrefetchScalarGridSpec(num_sc...  44 us
    pallas_call x1, Pallas kernels, project_out(): pl.pallas_call(out_kernel, grid_spec=pltpu.PrefetchScalarGridSpec(num_sca...  42.1 us
    pallas_call x1, Pallas kernels, matmul(): pl.pallas_call(functools.partial(mm_kernel, dims), grid_spec=pltpu.Prefet...  41.2 us
    pallas_call x2, Pallas kernels, wgrad(): pl.pallas_call(functools.partial(keep_kernel, axis), grid_spec=pltpu.Pref...  35.2 us
  transfers between devices with their start and end apart: 10, of which 5 were waited for; matrix products, arithmetic and copies ran while one was open for 2% of the time, Pallas kernels for 23%

commit v1 on v0

--- a/solution.py
+++ b/solution.py
@@ -110,21 +110,29 @@
     return pl.ds(m * rows + part * (rows // 2), rows // 2), pl.ds(pl.multiple_of(d * cols, cols), cols)
 
 
-def front_kernel(half, tok, wq, wkv, wo, gain, wcat, wo_full, hidden, means, inv_stds, proj, q_send, q_recv, o_send, o_recv, kv_send, kv_recv, local):
+def front_kernel(half, tok, grad, wq, wkv, wo, gain, wcat, wo_full, hidden, means, inv_stds, proj, grad_mixed, wbuf, obuf, kbuf, q_send, q_recv, o_send, o_recv, kv_send, kv_recv, local):
     d, _, x, c, yn, xn, pn = place()
     rows, cols = wq.shape
     depth, width = wo_full.shape[1], wo_full.shape[0]
     krows, pair = wkv.shape[0] // 2, wkv.shape[1]
+    part = width // 2
     entry_barrier((yn, xn, pn))
     k_here = lambda dd, cc: wcat.at[pl.ds(dd * 2 * krows + cc * krows, krows), pl.ds(width, pair)]
     k_out = remote(wkv.at[pl.ds(c * krows, krows), :], k_here(d, c), kv_send.at[0], kv_recv.at[0], yn)
     k_fwd = remote(k_here(1 - d, c), k_here(1 - d, c), kv_send.at[1], kv_recv.at[1], pn)
     k_own = pltpu.make_async_copy(wkv, wcat.at[pl.ds(d * 2 * krows, 2 * krows), pl.ds(width, pair)], local.at[2])
-    k_out.start()
     gather_q = Gather(wq, wcat, functools.partial(q_region, rows, cols), q_send, q_recv, local.at[0])
     gather_o = Gather(wo, wo_full, functools.partial(o_region, wo.shape[0], wo.shape[1]), o_send, o_recv, local.at[1])
     gather_q.start()
+    k_out.start()
     k_own.start()
+    mine = lambda *_: pl.ds(pl.multiple_of(x * part, part), part)
+    other = lambda *_: pl.ds(pl.multiple_of((1 - x) * part, part), part)
+    load_q0 = pltpu.make_async_copy(wcat.at[:, mine()], wbuf.at[0], local.at[3])
+    load_q1 = pltpu.make_async_copy(wcat.at[:, other()], wbuf.at[1], local.at[4])
+    load_kv = pltpu.make_async_copy(wcat.at[:, pl.ds(width, pair)], kbuf, local.at[5])
+    load_o0 = pltpu.make_async_copy(wo_full.at[mine(), :], obuf.at[0], local.at[6])
+    load_o1 = pltpu.make_async_copy(wo_full.at[other(), :], obuf.at[1], local.at[7])
 
     def norm_block(tok_blk, hid_blk, mean_blk, inv_blk):
         rows_f = tok_blk[...].astype(F32)
@@ -145,58 +153,46 @@
 
     big = 1024
 
-    def block(a, b, out):
-        out[...] = dot(a[...], b[...], NN).astype(BF16)
-
-    def run(col, cols_n, row_block, row_blocks):
-        span = pl.ds(pl.multiple_of(col, cols_n), cols_n)
+    def run(src, weight, dims, out):
+        def block(a, o):
+            o[...] = dot(a[...], weight[...], dims).astype(BF16)
+
         pltpu.emit_pipeline(
             block,
-            grid=(row_blocks,),
-            in_specs=[pl.BlockSpec((big, depth), lambda i: (row_block + i, 0)), pl.BlockSpec((depth, cols_n), lambda i: (0, 0))],
-            out_specs=[pl.BlockSpec((big, cols_n), lambda i: (row_block + i, 0))],
-        )(hidden, wcat.at[:, span], proj.at[:, span])
-
-    blocks = half // big
+            grid=(half // big,),
+            in_specs=[pl.BlockSpec((big, depth), lambda i: (i, 0))],
+            out_specs=[pl.BlockSpec((big, out.shape[1]), lambda i: (i, 0))],
+        )(src, out)
+
+    gather_q.middle()
+    gather_o.start()
+    gather_q.own_half()
+    load_q0.start()
     k_out.wait_recv()
     k_fwd.start()
     k_own.wait()
+    load_q0.wait()
+    run(hidden, wbuf.at[0], NN, proj.at[:, mine()])
+    gather_q.finish()
+    load_q1.start()
     k_fwd.wait_recv()
-    run(width, pair, 0, blocks)
-    gather_q.middle()
-    gather_o.start()
-    gather_q.own_half()
-    run(x * (width // 2), width // 2, 0, blocks)
-    gather_q.finish()
-    run((1 - x) * (width // 2), width // 2, 0, blocks // 2)
+    load_kv.start()
+    load_kv.wait()
+    run(hidden, kbuf, NN, proj.at[:, pl.ds(width, pair)])
+    load_q1.wait()
+    run(hidden, wbuf.at[1], NN, proj.at[:, other()])
     gather_o.middle()
-    run((1 - x) * (width // 2), width // 2, blocks // 2, blocks - blocks // 2)
     gather_o.own_half()
+    load_o0.start()
+    load_o0.wait()
+    own_grad = grad.at[pl.ds(c * half, half), :]
+    run(own_grad, obuf.at[0], NT, grad_mixed.at[:, mine()])
     gather_o.finish()
+    load_o1.start()
+    load_o1.wait()
+    run(own_grad, obuf.at[1], NT, grad_mixed.at[:, other()])
     k_out.wait_send()
     k_fwd.wait_send()
-
-
-def mm_kernel(dims, off, a, b, out):
-    out[...] = dot(a[...], b[...], dims).astype(BF16)
-
-
-def matmul(a, b, dims, rows, row_block, tile=1024):
-    depth = a.shape[1]
-    width = b.shape[1] if dims == NN else b.shape[0]
-    b_spec = pl.BlockSpec((depth, tile), lambda j, i, off: (0, j)) if dims == NN else pl.BlockSpec((tile, depth), lambda j, i, off: (j, 0))
-    return pl.pallas_call(
-        functools.partial(mm_kernel, dims),
-        grid_spec=pltpu.PrefetchScalarGridSpec(
-            num_scalar_prefetch=1,
-            grid=(width // tile, rows // tile),
-            in_specs=[pl.BlockSpec((tile, depth), lambda j, i, off: (off[0] + i, 0)), b_spec],
-            out_specs=pl.BlockSpec((tile, tile), lambda j, i, off: (i, j)),
-        ),
-        out_shape=jax.ShapeDtypeStruct((rows, width), BF16),
-        cost_estimate=pl.CostEstimate(flops=2 * rows * depth * width, bytes_accessed=2 * (rows * depth + depth * width + rows * width), transcendentals=0),
-        compiler_params=pltpu.CompilerParams(vmem_limit_bytes=LIMIT),
-    )(row_block, a, b)
 
 
 def attend_kernel(heads, head_dim, qkv_ref, do_ref, pos_c_ref, pos_r_ref, o_ref, dqkv_ref, seen, pt, dst):
@@ -264,68 +260,71 @@
     )(proj, grad_mixed, positions.reshape(seq, 1), positions.reshape(1, seq))
 
 
-def give_kernel(off, a, b, out):
-    part = dot(a[...], b[...], TN)
-
-    @pl.when(pl.program_id(2) == 0)
-    def _():
-        out[...] = part
-
-    @pl.when(pl.program_id(2) > 0)
-    def _():
-        out[...] += part
-
-
-def keep_kernel(axis, off, a, b, got, send, keep):
-    part = dot(a[...], b[...], TN)
-    k = pl.program_id(2)
-
-    def add(out):
-        @pl.when(k == 0)
-        def _():
-            out[...] = got[...] + part
-
-        @pl.when(k > 0)
-        def _():
-            out[...] += part
-
-    pl.when(pl.program_id(axis) == 0)(lambda: add(send))
-    pl.when(pl.program_id(axis) == 1)(lambda: add(keep))
-
-
-def wgrad(a, b, offs, shape, tiles, got=None, axis=None):
-    bm, bn, deep = tiles
+def give_kernel(count, off, a, *refs):
+    for b, out in zip(refs[:count], refs[count:]):
+        out[...] = dot(a[...], b[...], TN)
+
+
+def give(a, bs, offs, shape, widths, tile=512):
+    rows = a.shape[0]
     height, width = shape
-    grid = (height // bm, width // bn, a.shape[0] // deep)
-    half = lambda t, ax, off: jnp.where(t == 0, 1 - off[3], off[3]) if axis == ax else t
-    in_specs = [
-        pl.BlockSpec((deep, bm), lambda i, j, k, off: (k, off[0] + half(i, 0, off))),
-        pl.BlockSpec((deep, bn), lambda i, j, k, off: (off[1] + k, off[2] + half(j, 1, off))),
-    ]
-    cost = pl.CostEstimate(flops=2 * a.shape[0] * height * width, bytes_accessed=2 * a.shape[0] * (height + width), transcendentals=0)
-    params = pltpu.CompilerParams(vmem_limit_bytes=LIMIT)
-    if got is None:
-        return pl.pallas_call(
-            give_kernel,
-            grid_spec=pltpu.PrefetchScalarGridSpec(
-                num_scalar_prefetch=1, grid=grid, in_specs=in_specs, out_specs=pl.BlockSpec((bm, bn), lambda i, j, k, off: (i, j))
-            ),
-            out_shape=jax.ShapeDtypeStruct(shape, F32),
-            cost_estimate=cost,
-            compiler_params=params,
-        )(offs, a, b)
-    piece = pl.BlockSpec((bm, bn), lambda i, j, k, off: (0, 0))
+    wide = width // tile
+    blocks = [tile] + list(widths[1:])
+    b_specs = [pl.BlockSpec((rows, w), functools.partial(lambda n, i, j, off: (off[1], off[2 + n] + (j if n == 0 else 0)), n)) for n, w in enumerate(blocks)]
+    o_specs = [pl.BlockSpec((tile, w), functools.partial(lambda n, i, j, off: (i, j if n == 0 else 0), n)) for n, w in enumerate(blocks)]
     return pl.pallas_call(
-        functools.partial(keep_kernel, axis),
+        functools.partial(give_kernel, len(bs)),
         grid_spec=pltpu.PrefetchScalarGridSpec(
             num_scalar_prefetch=1,
-            grid=grid,
-            in_specs=in_specs + [pl.BlockSpec((bm, bn), lambda i, j, k, off: (half(i, 0, off), half(j, 1, off)))],
-            out_specs=[piece, piece],
+            grid=(height // tile, wide),
+            in_specs=[pl.BlockSpec((rows, tile), lambda i, j, off: (0, off[0] + i))] + b_specs,
+            out_specs=o_specs,
         ),
-        out_shape=[jax.ShapeDtypeStruct((bm, bn), F32)] * 2,
-        cost_estimate=cost,
-        compiler_params=params,
+        out_shape=[jax.ShapeDtypeStruct((height, w), F32) for w in widths],
+        cost_estimate=pl.CostEstimate(flops=2 * rows * height * sum(widths), bytes_accessed=2 * rows * (height + sum(widths)), transcendentals=0),
+        compiler_params=pltpu.CompilerParams(vmem_limit_bytes=LIMIT),
+    )(offs, a, *bs)
+
+
+def keep_kernel(half, off, a, b, got, send, keep):
+    step = pl.program_id(0)
+    value = got[...] + dot(a[...], b[...], TN)
+
+    @pl.when(step < half)
+    def _():
+        send[...] = value
+
+    @pl.when(step >= half)
+    def _():
+        keep[...] = value
+
+
+def keep(a, b, offs, shape, axis, got, tile=512):
+    rows = a.shape[0]
+    steps = shape[axis] // tile
+    half = steps // 2
+    turn = lambda t, off: jnp.where(t < half, (1 - off[3]) * half + t, off[3] * half + t - half)
+    at = (lambda t, off: (turn(t, off), 0)) if axis == 0 else (lambda t, off: (0, turn(t, off)))
+    line = (lambda t: (t, 0)) if axis == 0 else (lambda t: (0, t))
+    out = (shape[0] // 2, shape[1]) if axis == 0 else (shape[0], shape[1] // 2)
+    return pl.pallas_call(
+        functools.partial(keep_kernel, half),
+        grid_spec=pltpu.PrefetchScalarGridSpec(
+            num_scalar_prefetch=1,
+            grid=(steps,),
+            in_specs=[
+                pl.BlockSpec((rows, tile), lambda t, off: (0, off[0] + at(t, off)[0])),
+                pl.BlockSpec((rows, tile), lambda t, off: (off[1], off[2] + at(t, off)[1])),
+                pl.BlockSpec((tile, tile), at),
+            ],
+            out_specs=[
+                pl.BlockSpec((tile, tile), lambda t, off: line(jnp.minimum(t, half - 1))),
+                pl.BlockSpec((tile, tile), lambda t, off: line(jnp.maximum(t - half, 0))),
+            ],
+        ),
+        out_shape=[jax.ShapeDtypeStruct(out, F32)] * 2,
+        cost_estimate=pl.CostEstimate(flops=2 * rows * shape[0] * shape[1], bytes_accessed=2 * rows * sum(shape), transcendentals=0),
+        compiler_params=pltpu.CompilerParams(vmem_limit_bytes=LIMIT),
     )(offs, a, b, got)
 
 
@@ -457,10 +456,10 @@
             return lax.ppermute(a, "data", datas)
 
 
-        wcat, wo, hidden, means, inv_stds, proj = pl.pallas_call(
+        wcat, wo, hidden, means, inv_stds, proj, grad_mixed = pl.pallas_call(
             functools.partial(front_kernel, half),
-            in_specs=[ANY, VMEM, VMEM, VMEM, VMEM],
-            out_specs=[ANY] * 6,
+            in_specs=[ANY, ANY, VMEM, VMEM, VMEM, VMEM],
+            out_specs=[ANY] * 7,
             out_shape=[
                 jax.ShapeDtypeStruct((depth, width + pair), BF16),
                 jax.ShapeDtypeStruct((width, depth), BF16),
@@ -468,32 +467,30 @@
                 jax.ShapeDtypeStruct((half, 128), F32),
                 jax.ShapeDtypeStruct((half, 128), F32),
                 jax.ShapeDtypeStruct((half, width + pair), BF16),
+                jax.ShapeDtypeStruct((half, width), BF16),
             ],
-            scratch_shapes=[sems(9), sems(9), sems(9), sems(9), sems(2), sems(2), sems(3)],
+            scratch_shapes=[pltpu.VMEM((2, depth, width // 2), BF16), pltpu.VMEM((2, width // 2, depth), BF16), pltpu.VMEM((depth, pair), BF16)]
+            + [sems(9), sems(9), sems(9), sems(9), sems(2), sems(2), sems(8)],
             compiler_params=pltpu.CompilerParams(collective_id=0, has_side_effects=True, vmem_limit_bytes=LIMIT),
-        )(tok, wq_blk, wkv_blk, wo_blk, gain)
-
-        grad_mixed = matmul(grad, wo, NT, half, core * (half // 1024))
+        )(tok, grad, wq_blk, wkv_blk, wo_blk, gain)
+
         mixed, gqkv = attend(proj, grad_mixed, positions)
 
-        deep = 2048
         mine, other = 2 * x + c, 2 * x + 1 - c
-        row_o = c * (half // deep)
-        give_o = wgrad(mixed, grad, index(other, row_o, 0, 0), (piece, depth), (piece, depth // 2, deep))
+        (give_o,) = give(mixed, [grad], index(other, c, 0), (piece, depth), [depth])
         got_o = swap(give_o)
-        give_q = wgrad(after(hidden, give_o), gqkv, index(0, 0, other, 0), (depth, piece), (depth // 2, piece, deep))
+        give_q, part_kv = give(after(hidden, give_o), [gqkv, gqkv], index(0, 0, other, width // pair), (depth, piece), [piece, pair])
         got_q = swap(give_q)
-        part_kv = wgrad(after(hidden, give_q), gqkv, index(0, 0, width // pair, 0), (depth, pair), (depth // 2, pair, deep))
-        send_o, keep_o = wgrad(after(mixed, part_kv), grad, index(mine, row_o, 0, d), (piece, depth), (piece, depth // 2, deep), got_o, 1)
+        send_o, keep_o = keep(after(mixed, give_q), grad, index(mine, c, 0, d), (piece, depth), 1, got_o)
         data_o = cross(send_o)
-        send_q, keep_q = wgrad(after(hidden, send_o), gqkv, index(0, 0, mine, d), (depth, piece), (depth // 2, piece, deep), got_q, 0)
+        send_q, keep_q = keep(after(hidden, send_o), gqkv, index(0, 0, mine, d), (depth, piece), 0, got_q)
         data_q = cross(send_q)
 
         def halves(a, i, axis):
             size = a.shape[axis] // 2
             return lax.dynamic_slice_in_dim(a, i * size, size, axis), lax.dynamic_slice_in_dim(a, (1 - i) * size, size, axis)
 
-        kv_keep, kv_give = halves(part_kv, c, 1)
+        kv_keep, kv_give = halves(after(part_kv, send_o), c, 1)
         kv_sum = kv_keep + swap(kv_give)
         kv_keep, kv_give = halves(kv_sum, d, 0)
         kv_data = cross(kv_give)
@@ -507,7 +504,7 @@
         dx_got_0 = swap(dx_send)
         grad_w_query = (keep_q + data_q).astype(BF16)
         grad_w_kv = jnp.where(c == 0, jnp.concatenate([kv_cols, kv_other], axis=1), jnp.concatenate([kv_other, kv_cols], axis=1))
-        dx, dx_send, y = grad_tok(after(gqkv, dx_send, grad_w_query, grad_w_kv), wcat, gain, tok, means, inv_stds, core, 1, (dx, y, y_got))
+        dx, dx_send, y = grad_tok(after(gqkv, dx_send, grad_w_query), wcat, gain, tok, means, inv_stds, core, 1, (dx, y, y_got))
         dx_got_1 = swap(dx_send)
         dx = fill(dx, dx_got_0, core, 0)
         dx = fill(dx, dx_got_1, core, 1)

time: 517 us -> 511 us (0.988)
    pallas_call x7 -> x5, Pallas kernels: 221 us -> 217 us  [the longest x1 149 us: layer(): pl.pallas_call(functools.partial(front_kernel, half), in_specs=[ANY, ANY,...]
  transfers between devices with their start and end apart: 10 -> 10, of which waited for: 5 -> 3; matrix products, arithmetic and copies ran while one was open for 2% -> 2% of each run, Pallas kernels for 23% -> 25%
where the time goes in v1:
time: 511 us; the launch traced here: 504 us
  Pallas kernels  405 us (79%)
  waiting for transfers between devices  79.1 us (15%)
  other arithmetic  11.5 us (2%)
    pallas_call x1, Pallas kernels, layer(): pl.pallas_call(functools.partial(front_kernel, half), in_specs=[ANY, ANY,...  149 us
    pallas_call x2, Pallas kernels, grad_tok(): pl.pallas_call(functools.partial(grad_tok_kernel, earlier is not None), g...  67.7 us
    pallas_call x1, Pallas kernels, attend(): pl.pallas_call(functools.partial(attend_kernel, heads, head_dim), grid=(r...  66.6 us
    ppermute x3, waiting for transfers between devices, cross(): return lax.ppermute(a, 'data', datas)  65.9 us
    pallas_call x1, Pallas kernels, project_out(): pl.pallas_call(out_kernel, grid_spec=pltpu.PrefetchScalarGridSpec(num_sca...  42.2 us
    pallas_call x2, Pallas kernels, give(): pl.pallas_call(functools.partial(give_kernel, len(bs)), grid_spec=pltpu.P...  34.8 us
    pallas_call x2, Pallas kernels, keep(): pl.pallas_call(functools.partial(keep_kernel, half), grid_spec=pltpu.Pref...  32.3 us
    ppermute x7, waiting for transfers between devices, swap(): return lax.ppermute(a, 'model', cores)  13.2 us
  transfers between devices with their start and end apart: 10, of which 3 were waited for; matrix products, arithmetic and copies ran while one was open for 2% of the time, Pallas kernels for 25%

profile of v1, /device:TPU:0, one launch (start us, length us, event | category | flops | bytes accessed | tf_op | source)
XLA Modules:
  0.0 503.6 jit_solution(6347963535805867835)
XLA Ops:
  0.7 1.5 copy.16.pos_c_ref
  2.1 0.6 pad_add_fusion.2.off
  2.7 149.5 %shard_map.110 = (bf16[2048,2304]{1,0:T(8,128)(2,1)}, bf16[2048,2048]{1,0:T(8,128)(2,1)}, bf16[4096,2048]{1,0:T(8,128)(2,1)}, f32[4096,128]{1,0:T(8,128)}, f32[4...) custom-call(bf16[8192,2048]{1,0:T(8,128)(2,1)} %tok.5, bf16[8192,2048]{1,0:T(8,128)(2,1)} %b.1, ...), custom_call_target="tpu_custom_call" | custom-call | tf_op jit(solution)/shard_map/pallas_call | solution.py:459
  152.2 66.6 %shard_map.111 = (bf16[4096,2048]{1,0:T(8,128)(2,1)}, bf16[4096,2304]{1,0:T(8,128)(2,1)}) custom-call(bf16[4096,2304]{1,0:T(8,128)(2,1)} %get-tuple-element.34.qkv_ref, bf16[4096,2048]{1,0:T(8,128)(2,1)} %get-tuple-element.35.do_ref, s32[256,1]{1,0:T(8,128)} %copy.16.pos_c_ref, s32[1,256]{1,0:T(1,128)} %bitcast.11), custom_call_target="tpu_custom_call" | custom-call | flops 25769803776 | bytes 67108864 | tf_op jit(solution)/shard_map/pallas_call | solution.py:251
  218.8 14.9 %shard_map.112 = f32[512,2048]{1,0:T(8,128)} custom-call(s32[3]{0:T(128)} %pad_add_fusion.2.off, bf16[4096,2048]{1,0:T(8,128)(2,1)} %get-tuple-element.47.a, bf16[8192,2048]{1,0:T(8,128)(2,1)} %b.1), custom_call_target="tpu_custom_call" | custom-call | flops 8589934592 | bytes 20971520 | tf_op jit(solution)/shard_map/pallas_call | solution.py:275
  233.7 0.4 collective-permute-start
  234.1 0.6 fusion.1
  234.7 19.9 %shard_map.113 = (f32[2048,512]{1,0:T(8,128)}, f32[2048,256]{1,0:T(8,128)}) custom-call(s32[4]{0:T(128)} %get-tuple-element.63.off, bf16[4096,2048]{1,0:T(8,128)(2,1)} %get-tuple-element.43.a, bf16[4096,2304]{1,0:T(8,128)(2,1)} %get-tuple-element.57.refs_0_.refs_1_.b.gqkv, bf16[4096,2304]{1,0:T(8,128)(2,1)} %get-tuple-element.57.refs_0_.refs_1_.b.gqkv), custom_call_target="tpu_custom_call" | custom-call | flops 12884901888 | bytes 23068672 | tf_op jit(solution)/shard_map/pallas_call | solution.py:275
  254.6 0.1 collective-permute-start.1
  254.7 0.6 add_add_fusion.off
  255.3 0.0 collective-permute-done.got
  255.3 16.2 %shard_map.114 = (f32[512,1024]{1,0:T(8,128)}, f32[512,1024]{1,0:T(8,128)}) custom-call(s32[4]{0:T(128)} %add_add_fusion.off, bf16[4096,2048]{1,0:T(8,128)(2,1)} %get-tuple-element.47.a, bf16[8192,2048]{1,0:T(8,128)(2,1)} %b.1, f32[512,2048]{1,0:T(8,128)} %collective-permute-done.got), custom_call_target="tpu_custom_call" | custom-call | flops 8589934592 | bytes 20971520 | tf_op jit(solution)/shard_map/pallas_call | solution.py:310
  271.5 1.3 constant_dynamic-slice_fusion.1
  272.8 0.4 collective-permute-start.2
  273.3 0.0 collective-permute-done.1.got
  273.3 16.1 %shard_map.115 = (f32[1024,512]{1,0:T(8,128)}, f32[1024,512]{1,0:T(8,128)}) custom-call(s32[4]{0:T(128)} %get-tuple-element.64.off, bf16[4096,2048]{1,0:T(8,128)(2,1)} %get-tuple-element.43.a, bf16[4096,2304]{1,0:T(8,128)(2,1)} %get-tuple-element.57.refs_0_.refs_1_.b.gqkv, f32[2048,512]{1,0:T(8,128)} %collective-permute-done.1.got), custom_call_target="tpu_custom_call" | custom-call | flops 8589934592 | bytes 20971520 | tf_op jit(solution)/shard_map/pallas_call | solution.py:310
  289.3 0.0 collective-permute-done.2
  289.3 1.6 dynamic-slice_add_fusion
  291.0 42.2 %shard_map.116 = (bf16[8192,2048]{1,0:T(8,128)(2,1)}, bf16[4096,2048]{1,0:T(8,128)(2,1)}) custom-call(s32[1]{0:T(128)} %bitcast.off, bf16[4096,2048]{1,0:T(8,128)(2,1)} %get-tuple-element.47.a, bf16[2048,2048]{1,0:T(8,128)(2,1)} %get-tuple-element.48.b), custom_call_target="tpu_custom_call" | custom-call | flops 34359738368 | bytes 50331648 | tf_op jit(solution)/shard_map/pallas_call | solution.py:341
  333.2 0.1 collective-permute-start.6
  333.3 0.9 collective-permute-start.3
  334.3 1.1 collective-permute-start.4
  335.4 0.9 collective-permute-start.5
  336.3 56.9 %collective-permute-done.4 = f32[1024,128]{1,0:T(8,128)S(1)} collective-permute-done((f32[1024,128]{1,0:T(8,128)S(1)}, f32[1024,128]{1,0:T(8,128)S(1)}, u32[]{:S(2)}, u32[]{:S(2)}) %collective-permute-start.4) | collective-permute-done | bytes 524320 | tf_op jit(solution)/shard_map/ppermute | solution.py:456
  393.2 0.1 add_convert_fusion.2
  393.3 0.0 collective-permute-done.3
  393.3 3.5 add_convert_fusion.1
  396.8 32.0 %shard_map.117 = (bf16[8192,2048]{1,0:T(8,128)(2,1)}, bf16[2048,2048]{1,0:T(8,128)(2,1)}) custom-call(s32[1]{0:T(128)} %bitcast.off, bf16[4096,2304]{1,0:T(8,128)(2,1)} %get-tuple-element.57.refs_0_.refs_1_.b.gqkv, bf16[2048,2304]{1,0:T(8,128)(2,1)} %get-tuple-element.52.wcat, f32[1,2048]{1,0:T(1,128)} %bitcast.8, bf16[8192,2048]{1,0:T(8,128)(2,1)} %tok.5, ...), custom_call_target="tpu_custom_call" | custom-call | flops 19327352832 | bytes 41943040 | tf_op jit(solution)/shard_map/pallas_call | solution.py:397
  428.8 0.0 collective-permute-start.8
  428.8 8.9 %collective-permute-done.5 = f32[1024,512]{1,0:T(8,128)} collective-permute-done((f32[1024,512]{1,0:T(8,128)}, f32[1024,512]{1,0:T(8,128)}, u32[]{:S(2)}, u32[]{:S(2)}) %collective-permute-start.5) | collective-permute-done | bytes 2097184 | tf_op jit(solution)/shard_map/ppermute | solution.py:456
  437.7 3.5 add_convert_fusion
  441.3 0.0 collective-permute-done.6.refs_0_
  441.3 35.7 %shard_map.118 = (bf16[8192,2048]{1,0:T(8,128)(2,1)}, bf16[2048,2048]{1,0:T(8,128)(2,1)}, bf16[8192,2048]{1,0:T(8,128)(2,1)}) custom-call(s32[1]{0:T(128)} %bitcast.off, bf16[4096,2304]{1,0:T(8,128)(2,1)} %get-tuple-element.57.refs_0_.refs_1_.b.gqkv, bf16[2048,2304]{1,0:T(8,128)(2,1)} %get-tuple-element.52.wcat, ...), custom_call_target="tpu_custom_call", output_to_operand_aliasing={{0}: (8, {}), {2}: (9, {})} | custom-call | flops 19327352832 | bytes 41943040 | tf_op jit(solution)/shard_map/pallas_call | solution.py:397
  477.0 0.0 collective-permute-start.7
  477.0 0.5 collective-permute-start.9
  477.5 13.2 %collective-permute-done.9 = bf16[1024,128]{1,0:T(8,128)(2,1)S(1)} collective-permute-done((bf16[1024,128]{1,0:T(8,128)(2,1)S(1)}, bf16[1024,128]{1,0:T(8,128)(2,1)S(1)}, u32[]{:S(2)}, u32[]{:S(2)}) %collective-permute-start.9) | collective-permute-done | bytes 262176 | tf_op jit(solution)/shard_map/ppermute | solution.py:453
  490.7 1.0 maximum_select_fusion
  491.7 0.0 collective-permute-done.8.got
  491.7 5.9 %shard_map.119._ = bf16[8192,2048]{1,0:T(8,128)(2,1)} custom-call(s32[1]{0:T(128)} %bitcast.off, bf16[2048,2048]{1,0:T(8,128)(2,1)} %collective-permute-done.8.got, bf16[8192,2048]{1,0:T(8,128)(2,1)} %get-tuple-element.62._), custom_call_target="tpu_custom_call", output_to_operand_aliasing={{}: (2, {})} | custom-call | flops 4194304 | bytes 16777216 | tf_op jit(solution)/shard_map/pallas_call | solution.py:414
  497.6 0.0 collective-permute-done.7.got
  497.6 5.9 %shard_map.120 = bf16[8192,2048]{1,0:T(8,128)(2,1)} custom-call(s32[1]{0:T(128)} %bitcast.off, bf16[2048,2048]{1,0:T(8,128)(2,1)} %collective-permute-done.7.got, bf16[8192,2048]{1,0:T(8,128)(2,1)} %shard_map.119._), custom_call_target="tpu_custom_call", output_to_operand_aliasing={{}: (2, {})} | custom-call | flops 4194304 | bytes 16777216 | tf_op jit(solution)/shard_map/pallas_call | solution.py:414
  (2 shorter events, 0.0 us)
Async XLA Ops:
  233.7 21.6 %collective-permute-start = (f32[512,2048]{1,0:T(8,128)}, f32[512,2048]{1,0:T(8,128)}, u32[]{:S(2)}, u32[]{:S(2)}) collective-permute-start(f32[512,2048]{1,0:T(8,128)} %shard_map.112), channel_id=1, source_target_pairs={{0,1},{1,0},{2,3},{3,2},{4,5},{5,4},{6,7},{7,6}} | collective-permute-start | bytes 12582920 | tf_op jit(solution)/shard_map/ppermute | solution.py:453
  254.6 18.7 %collective-permute-start.1 = (f32[2048,512]{1,0:T(8,128)}, f32[2048,512]{1,0:T(8,128)}, u32[]{:S(2)}, u32[]{:S(2)}) collective-permute-start(f32[2048,512]{1,0:T(8,128)} %get-tuple-element.40), channel_id=1, source_target_pairs={{0,1},{1,0},{2,3},{3,2},{4,5},{5,4},{6,7},{7,6}} | collective-permute-start | bytes 12582920 | tf_op jit(solution)/shard_map/ppermute | solution.py:453
  272.8 16.5 %collective-permute-start.2 = (f32[2048,128]{1,0:T(8,128)S(1)}, f32[2048,128]{1,0:T(8,128)}, u32[]{:S(2)}, u32[]{:S(2)}) collective-permute-start(f32[2048,128]{1,0:T(8,128)S(1)} %constant_dynamic-slice_fusion.1), channel_id=1, source_target_pairs={{0,1},{1,0},{2,3},{3,2},{4,5},{5,4},{6,7},{7,6}} | collective-permute-start | bytes 3145736 | tf_op jit(solution)/shard_map/ppermute | solution.py:453
  333.2 108.1 %collective-permute-start.6 = (bf16[4096,2048]{1,0:T(8,128)(2,1)}, bf16[4096,2048]{1,0:T(8,128)(2,1)}, u32[]{:S(2)}, u32[]{:S(2)}) collective-permute-start(bf16[4096,2048]{1,0:T(8,128)(2,1)} %get-tuple-element.49), channel_id=1, source_target_pairs={{0,1},{1,0},{2,3},{3,2},{4,5},{5,4},{6,7},{7,6}} | collective-permute-start | bytes 50331656 | tf_op jit(solution)/shard_map/ppermute | solution.py:453
  333.3 60.0 %collective-permute-start.3 = (f32[512,1024]{1,0:T(8,128)}, f32[512,1024]{1,0:T(8,128)}, u32[]{:S(2)}, u32[]{:S(2)}) collective-permute-start(f32[512,1024]{1,0:T(8,128)} %get-tuple-element.42), channel_id=1, source_target_pairs={{0,4},{4,0},{1,5},{5,1},{2,6},{6,2},{3,7},{7,3}} | collective-permute-start | bytes 6291464 | tf_op jit(solution)/shard_map/ppermute | solution.py:456
  334.3 59.0 %collective-permute-start.4 = (f32[1024,128]{1,0:T(8,128)S(1)}, f32[1024,128]{1,0:T(8,128)S(1)}, u32[]{:S(2)}, u32[]{:S(2)}) collective-permute-start(f32[1024,128]{1,0:T(8,128)S(1)} %constant_dynamic-slice_fusion), channel_id=1, source_target_pairs={{0,4},{4,0},{1,5},{5,1},{2,6},{6,2},{3,7},{7,3}} | collective-permute-start | bytes 1572872 | tf_op jit(solution)/shard_map/ppermute | solution.py:456
  335.4 102.4 %collective-permute-start.5 = (f32[1024,512]{1,0:T(8,128)}, f32[1024,512]{1,0:T(8,128)}, u32[]{:S(2)}, u32[]{:S(2)}) collective-permute-start(f32[1024,512]{1,0:T(8,128)} %get-tuple-element.44), channel_id=1, source_target_pairs={{0,4},{4,0},{1,5},{5,1},{2,6},{6,2},{3,7},{7,3}} | collective-permute-start | bytes 6291464 | tf_op jit(solution)/shard_map/ppermute | solution.py:456
  428.8 62.9 %collective-permute-start.8 = (bf16[2048,2048]{1,0:T(8,128)(2,1)}, bf16[2048,2048]{1,0:T(8,128)(2,1)}, u32[]{:S(2)}, u32[]{:S(2)}) collective-permute-start(bf16[2048,2048]{1,0:T(8,128)(2,1)} %get-tuple-element.55), channel_id=1, source_target_pairs={{0,1},{1,0},{2,3},{3,2},{4,5},{5,4},{6,7},{7,6}} | collective-permute-start | bytes 25165832 | tf_op jit(solution)/shard_map/ppermute | solution.py:453
  477.0 20.6 %collective-permute-start.7 = (bf16[2048,2048]{1,0:T(8,128)(2,1)}, bf16[2048,2048]{1,0:T(8,128)(2,1)}, u32[]{:S(2)}, u32[]{:S(2)}) collective-permute-start(bf16[2048,2048]{1,0:T(8,128)(2,1)} %get-tuple-element.61), channel_id=1, source_target_pairs={{0,1},{1,0},{2,3},{3,2},{4,5},{5,4},{6,7},{7,6}} | collective-permute-start | bytes 25165832 | tf_op jit(solution)/shard_map/ppermute | solution.py:453
  477.0 13.7 %collective-permute-start.9 = (bf16[1024,128]{1,0:T(8,128)(2,1)S(1)}, bf16[1024,128]{1,0:T(8,128)(2,1)S(1)}, u32[]{:S(2)}, u32[]{:S(2)}) collective-permute-start(bf16[1024,128]{1,0:T(8,128)(2,1)S(1)} %add_convert_fusion.2), channel_id=1, source_target_pairs={{0,1},{1,0},{2,3},{3,2},{4,5},{5,4},{6,7},{7,6}} | collective-permute-start | bytes 786440 | tf_op jit(solution)/shard_map/ppermute | solution.py:453

commit v2 on v1

--- a/solution.py
+++ b/solution.py
@@ -123,8 +123,8 @@
     k_own = pltpu.make_async_copy(wkv, wcat.at[pl.ds(d * 2 * krows, 2 * krows), pl.ds(width, pair)], local.at[2])
     gather_q = Gather(wq, wcat, functools.partial(q_region, rows, cols), q_send, q_recv, local.at[0])
     gather_o = Gather(wo, wo_full, functools.partial(o_region, wo.shape[0], wo.shape[1]), o_send, o_recv, local.at[1])
+    k_out.start()
     gather_q.start()
-    k_out.start()
     k_own.start()
     mine = lambda *_: pl.ds(pl.multiple_of(x * part, part), part)
     other = lambda *_: pl.ds(pl.multiple_of((1 - x) * part, part), part)
@@ -164,21 +164,21 @@
             out_specs=[pl.BlockSpec((big, out.shape[1]), lambda i: (i, 0))],
         )(src, out)
 
+    k_out.wait_recv()
+    k_fwd.start()
+    k_own.wait()
+    k_fwd.wait_recv()
+    load_kv.start()
+    load_kv.wait()
+    run(hidden, kbuf, NN, proj.at[:, pl.ds(width, pair)])
     gather_q.middle()
     gather_o.start()
     gather_q.own_half()
     load_q0.start()
-    k_out.wait_recv()
-    k_fwd.start()
-    k_own.wait()
     load_q0.wait()
     run(hidden, wbuf.at[0], NN, proj.at[:, mine()])
     gather_q.finish()
     load_q1.start()
-    k_fwd.wait_recv()
-    load_kv.start()
-    load_kv.wait()
-    run(hidden, kbuf, NN, proj.at[:, pl.ds(width, pair)])
     load_q1.wait()
     run(hidden, wbuf.at[1], NN, proj.at[:, other()])
     gather_o.middle()
@@ -476,35 +476,34 @@
 
         mixed, gqkv = attend(proj, grad_mixed, positions)
 
+        def halves(a, i, axis):
+            size = a.shape[axis] // 2
+            return lax.dynamic_slice_in_dim(a, i * size, size, axis), lax.dynamic_slice_in_dim(a, (1 - i) * size, size, axis)
+
         mine, other = 2 * x + c, 2 * x + 1 - c
         (give_o,) = give(mixed, [grad], index(other, c, 0), (piece, depth), [depth])
         got_o = swap(give_o)
         give_q, part_kv = give(after(hidden, give_o), [gqkv, gqkv], index(0, 0, other, width // pair), (depth, piece), [piece, pair])
         got_q = swap(give_q)
+        kv_keep, kv_give = halves(part_kv, c, 1)
+        kv_got = swap(kv_give)
         send_o, keep_o = keep(after(mixed, give_q), grad, index(mine, c, 0, d), (piece, depth), 1, got_o)
         data_o = cross(send_o)
-        send_q, keep_q = keep(after(hidden, send_o), gqkv, index(0, 0, mine, d), (depth, piece), 0, got_q)
+        kv_keep, kv_give = halves(kv_keep + kv_got, d, 0)
+        kv_data = cross(kv_give)
+        send_q, keep_q = keep(after(hidden, send_o, kv_give), gqkv, index(0, 0, mine, d), (depth, piece), 0, got_q)
         data_q = cross(send_q)
 
-        def halves(a, i, axis):
-            size = a.shape[axis] // 2
-            return lax.dynamic_slice_in_dim(a, i * size, size, axis), lax.dynamic_slice_in_dim(a, (1 - i) * size, size, axis)
-
-        kv_keep, kv_give = halves(after(part_kv, send_o), c, 1)
-        kv_sum = kv_keep + swap(kv_give)
-        kv_keep, kv_give = halves(kv_sum, d, 0)
-        kv_data = cross(kv_give)
-
-        y, y_send = project_out(after(mixed, send_q, kv_sum), wo, core)
+        y, y_send = project_out(after(mixed, send_q), wo, core)
         y_got = swap(y_send)
+        grad_w_out = (keep_o + data_o).astype(BF16)
+        dx, dx_send = grad_tok(after(gqkv, y_send, grad_w_out), wcat, gain, tok, means, inv_stds, core, 0)
+        dx_got_0 = swap(dx_send)
         kv_cols = (kv_keep + kv_data).astype(BF16)
         kv_other = swap(kv_cols)
-        grad_w_out = (keep_o + data_o).astype(BF16)
-        dx, dx_send = grad_tok(after(gqkv, y_send, grad_w_out, kv_cols), wcat, gain, tok, means, inv_stds, core, 0)
-        dx_got_0 = swap(dx_send)
         grad_w_query = (keep_q + data_q).astype(BF16)
         grad_w_kv = jnp.where(c == 0, jnp.concatenate([kv_cols, kv_other], axis=1), jnp.concatenate([kv_other, kv_cols], axis=1))
-        dx, dx_send, y = grad_tok(after(gqkv, dx_send, grad_w_query), wcat, gain, tok, means, inv_stds, core, 1, (dx, y, y_got))
+        dx, dx_send, y = grad_tok(after(gqkv, dx_send, grad_w_query, kv_cols), wcat, gain, tok, means, inv_stds, core, 1, (dx, y, y_got))
         dx_got_1 = swap(dx_send)
         dx = fill(dx, dx_got_0, core, 0)
         dx = fill(dx, dx_got_1, core, 1)

time: 511 us -> 518 us (1.014)
  waiting for transfers between devices: 79.1 us -> 87.4 us
    ppermute x7, waiting for transfers between devices: 13.2 us -> 19.8 us  [swap(): return lax.ppermute(a, 'model', cores)]
  transfers between devices with their start and end apart: 10 -> 10, of which waited for: 3 -> 4; matrix products, arithmetic and copies ran while one was open for 2% -> 2% of each run, Pallas kernels for 25% -> 22%
where the time goes in v2:
time: 518 us; the launch traced here: 510 us
  Pallas kernels  402 us (78%)
  waiting for transfers between devices  87.4 us (17%)
  other arithmetic  11.6 us (2%)
  starting transfers between devices  5.28 us (1%)
    pallas_call x1, Pallas kernels, layer(): pl.pallas_call(functools.partial(front_kernel, half), in_specs=[ANY, ANY,...  147 us
    pallas_call x2, Pallas kernels, grad_tok(): pl.pallas_call(functools.partial(grad_tok_kernel, earlier is not None), g...  67.7 us
    ppermute x3, waiting for transfers between devices, cross(): return lax.ppermute(a, 'data', datas)  67.6 us
    pallas_call x1, Pallas kernels, attend(): pl.pallas_call(functools.partial(attend_kernel, heads, head_dim), grid=(r...  66.6 us
    pallas_call x1, Pallas kernels, project_out(): pl.pallas_call(out_kernel, grid_spec=pltpu.PrefetchScalarGridSpec(num_sca...  42.1 us
    pallas_call x2, Pallas kernels, give(): pl.pallas_call(functools.partial(give_kernel, len(bs)), grid_spec=pltpu.P...  34.9 us
    pallas_call x2, Pallas kernels, keep(): pl.pallas_call(functools.partial(keep_kernel, half), grid_spec=pltpu.Pref...  32.2 us
    ppermute x7, waiting for transfers between devices, swap(): return lax.ppermute(a, 'model', cores)  19.8 us
  transfers between devices with their start and end apart: 10, of which 4 were waited for; matrix products, arithmetic and copies ran while one was open for 2% of the time, Pallas kernels for 22%

profile of v2, /device:TPU:0, one launch (start us, length us, event | category | flops | bytes accessed | tf_op | source)
XLA Modules:
  0.0 510.1 jit_solution(10082205319369175127)
XLA Ops:
  0.6 1.5 copy.16.pos_c_ref
  2.1 0.6 pad_add_fusion.2.off
  2.7 146.8 %shard_map.110 = (bf16[2048,2304]{1,0:T(8,128)(2,1)}, bf16[2048,2048]{1,0:T(8,128)(2,1)}, bf16[4096,2048]{1,0:T(8,128)(2,1)}, f32[4096,128]{1,0:T(8,128)}, f32[4...) custom-call(bf16[8192,2048]{1,0:T(8,128)(2,1)} %tok.5, bf16[8192,2048]{1,0:T(8,128)(2,1)} %b.1, ...), custom_call_target="tpu_custom_call" | custom-call | tf_op jit(solution)/shard_map/pallas_call | solution.py:459
  149.5 66.6 %shard_map.111 = (bf16[4096,2048]{1,0:T(8,128)(2,1)}, bf16[4096,2304]{1,0:T(8,128)(2,1)}) custom-call(bf16[4096,2304]{1,0:T(8,128)(2,1)} %get-tuple-element.33.qkv_ref, bf16[4096,2048]{1,0:T(8,128)(2,1)} %get-tuple-element.34.do_ref, s32[256,1]{1,0:T(8,128)} %copy.16.pos_c_ref, s32[1,256]{1,0:T(1,128)} %bitcast.11), custom_call_target="tpu_custom_call" | custom-call | flops 25769803776 | bytes 67108864 | tf_op jit(solution)/shard_map/pallas_call | solution.py:251
  216.1 14.9 %shard_map.112 = f32[512,2048]{1,0:T(8,128)} custom-call(s32[3]{0:T(128)} %pad_add_fusion.2.off, bf16[4096,2048]{1,0:T(8,128)(2,1)} %get-tuple-element.45.a, bf16[8192,2048]{1,0:T(8,128)(2,1)} %b.1), custom_call_target="tpu_custom_call" | custom-call | flops 8589934592 | bytes 20971520 | tf_op jit(solution)/shard_map/pallas_call | solution.py:275
  231.1 0.4 collective-permute-start
  231.4 0.7 fusion.1
  232.1 20.0 %shard_map.113 = (f32[2048,512]{1,0:T(8,128)}, f32[2048,256]{1,0:T(8,128)}) custom-call(s32[4]{0:T(128)} %get-tuple-element.61.off, bf16[4096,2048]{1,0:T(8,128)(2,1)} %get-tuple-element.43.a, bf16[4096,2304]{1,0:T(8,128)(2,1)} %get-tuple-element.55.refs_0_.refs_1_.b.gqkv, bf16[4096,2304]{1,0:T(8,128)(2,1)} %get-tuple-element.55.refs_0_.refs_1_.b.gqkv), custom_call_target="tpu_custom_call" | custom-call | flops 12884901888 | bytes 23068672 | tf_op jit(solution)/shard_map/pallas_call | solution.py:275
  252.2 0.1 collective-permute-start.2
  252.3 1.3 constant_dynamic-slice_fusion.1
  253.6 0.4 collective-permute-start.1
  254.0 0.6 add_add_fusion.off
  254.6 6.6 %collective-permute-done.1 = f32[2048,128]{1,0:T(8,128)} collective-permute-done((f32[2048,128]{1,0:T(8,128)S(1)}, f32[2048,128]{1,0:T(8,128)}, u32[]{:S(2)}, u32[]{:S(2)}) %collective-permute-start.1) | collective-permute-done | bytes 1048608 | tf_op jit(solution)/shard_map/ppermute | solution.py:453
  261.2 1.6 dynamic-slice_add_fusion
  262.9 0.0 collective-permute-done.got
  262.9 16.1 %shard_map.114 = (f32[512,1024]{1,0:T(8,128)}, f32[512,1024]{1,0:T(8,128)}) custom-call(s32[4]{0:T(128)} %add_add_fusion.off, bf16[4096,2048]{1,0:T(8,128)(2,1)} %get-tuple-element.45.a, bf16[8192,2048]{1,0:T(8,128)(2,1)} %b.1, f32[512,2048]{1,0:T(8,128)} %collective-permute-done.got), custom_call_target="tpu_custom_call" | custom-call | flops 8589934592 | bytes 20971520 | tf_op jit(solution)/shard_map/pallas_call | solution.py:310
  279.0 0.0 collective-permute-done.2.got
  279.0 16.1 %shard_map.115 = (f32[1024,512]{1,0:T(8,128)}, f32[1024,512]{1,0:T(8,128)}) custom-call(s32[4]{0:T(128)} %get-tuple-element.62.off, bf16[4096,2048]{1,0:T(8,128)(2,1)} %get-tuple-element.43.a, bf16[4096,2304]{1,0:T(8,128)(2,1)} %get-tuple-element.55.refs_0_.refs_1_.b.gqkv, f32[2048,512]{1,0:T(8,128)} %collective-permute-done.2.got), custom_call_target="tpu_custom_call" | custom-call | flops 8589934592 | bytes 20971520 | tf_op jit(solution)/shard_map/pallas_call | solution.py:310
  295.1 42.1 %shard_map.116 = (bf16[8192,2048]{1,0:T(8,128)(2,1)}, bf16[4096,2048]{1,0:T(8,128)(2,1)}) custom-call(s32[1]{0:T(128)} %bitcast.off, bf16[4096,2048]{1,0:T(8,128)(2,1)} %get-tuple-element.45.a, bf16[2048,2048]{1,0:T(8,128)(2,1)} %get-tuple-element.46.b), custom_call_target="tpu_custom_call" | custom-call | flops 34359738368 | bytes 50331648 | tf_op jit(solution)/shard_map/pallas_call | solution.py:341
  337.2 0.1 collective-permute-start.6
  337.4 1.5 collective-permute-start.3
  338.9 0.5 collective-permute-start.5
  339.4 57.3 %collective-permute-done.5 = f32[1024,128]{1,0:T(8,128)S(1)} collective-permute-done((f32[1024,128]{1,0:T(8,128)S(1)}, f32[1024,128]{1,0:T(8,128)S(1)}, u32[]{:S(2)}, u32[]{:S(2)}) %collective-permute-start.5) | collective-permute-done | bytes 524320 | tf_op jit(solution)/shard_map/ppermute | solution.py:456
  396.7 0.1 add_convert_fusion.2
  396.8 1.7 collective-permute-start.4
  398.4 0.0 collective-permute-done.3
  398.4 3.5 add_convert_fusion.1
  401.9 32.0 %shard_map.117 = (bf16[8192,2048]{1,0:T(8,128)(2,1)}, bf16[2048,2048]{1,0:T(8,128)(2,1)}) custom-call(s32[1]{0:T(128)} %bitcast.off, bf16[4096,2304]{1,0:T(8,128)(2,1)} %get-tuple-element.55.refs_0_.refs_1_.b.gqkv, bf16[2048,2304]{1,0:T(8,128)(2,1)} %get-tuple-element.50.wcat, f32[1,2048]{1,0:T(1,128)} %bitcast.8, bf16[8192,2048]{1,0:T(8,128)(2,1)} %tok.5, ...), custom_call_target="tpu_custom_call" | custom-call | flops 19327352832 | bytes 41943040 | tf_op jit(solution)/shard_map/pallas_call | solution.py:397
  433.9 0.0 collective-permute-start.8
  433.9 10.3 %collective-permute-done.4 = f32[1024,512]{1,0:T(8,128)} collective-permute-done((f32[1024,512]{1,0:T(8,128)}, f32[1024,512]{1,0:T(8,128)}, u32[]{:S(2)}, u32[]{:S(2)}) %collective-permute-start.4) | collective-permute-done | bytes 2097184 | tf_op jit(solution)/shard_map/ppermute | solution.py:456
  444.2 3.5 add_convert_fusion
  447.7 0.0 collective-permute-done.6.refs_0_
  447.7 35.7 %shard_map.118 = (bf16[8192,2048]{1,0:T(8,128)(2,1)}, bf16[2048,2048]{1,0:T(8,128)(2,1)}, bf16[8192,2048]{1,0:T(8,128)(2,1)}) custom-call(s32[1]{0:T(128)} %bitcast.off, bf16[4096,2304]{1,0:T(8,128)(2,1)} %get-tuple-element.55.refs_0_.refs_1_.b.gqkv, bf16[2048,2304]{1,0:T(8,128)(2,1)} %get-tuple-element.50.wcat, ...), custom_call_target="tpu_custom_call", output_to_operand_aliasing={{0}: (8, {}), {2}: (9, {})} | custom-call | flops 19327352832 | bytes 41943040 | tf_op jit(solution)/shard_map/pallas_call | solution.py:397
  483.4 0.0 collective-permute-start.7
  483.4 0.5 collective-permute-start.9
  483.9 13.2 %collective-permute-done.9 = bf16[1024,128]{1,0:T(8,128)(2,1)S(1)} collective-permute-done((bf16[1024,128]{1,0:T(8,128)(2,1)S(1)}, bf16[1024,128]{1,0:T(8,128)(2,1)S(1)}, u32[]{:S(2)}, u32[]{:S(2)}) %collective-permute-start.9) | collective-permute-done | bytes 262176 | tf_op jit(solution)/shard_map/ppermute | solution.py:453
  497.2 1.0 maximum_select_fusion
  498.1 0.0 collective-permute-done.8.got
  498.1 5.9 %shard_map.119._ = bf16[8192,2048]{1,0:T(8,128)(2,1)} custom-call(s32[1]{0:T(128)} %bitcast.off, bf16[2048,2048]{1,0:T(8,128)(2,1)} %collective-permute-done.8.got, bf16[8192,2048]{1,0:T(8,128)(2,1)} %get-tuple-element.60._), custom_call_target="tpu_custom_call", output_to_operand_aliasing={{}: (2, {})} | custom-call | flops 4194304 | bytes 16777216 | tf_op jit(solution)/shard_map/pallas_call | solution.py:414
  504.0 0.0 collective-permute-done.7.got
  504.0 5.9 %shard_map.120 = bf16[8192,2048]{1,0:T(8,128)(2,1)} custom-call(s32[1]{0:T(128)} %bitcast.off, bf16[2048,2048]{1,0:T(8,128)(2,1)} %collective-permute-done.7.got, bf16[8192,2048]{1,0:T(8,128)(2,1)} %shard_map.119._), custom_call_target="tpu_custom_call", output_to_operand_aliasing={{}: (2, {})} | custom-call | flops 4194304 | bytes 16777216 | tf_op jit(solution)/shard_map/pallas_call | solution.py:414
  (2 shorter events, 0.0 us)
Async XLA Ops:
  231.1 31.8 %collective-permute-start = (f32[512,2048]{1,0:T(8,128)}, f32[512,2048]{1,0:T(8,128)}, u32[]{:S(2)}, u32[]{:S(2)}) collective-permute-start(f32[512,2048]{1,0:T(8,128)} %shard_map.112), channel_id=1, source_target_pairs={{0,1},{1,0},{2,3},{3,2},{4,5},{5,4},{6,7},{7,6}} | collective-permute-start | bytes 12582920 | tf_op jit(solution)/shard_map/ppermute | solution.py:453
  252.2 26.9 %collective-permute-start.2 = (f32[2048,512]{1,0:T(8,128)}, f32[2048,512]{1,0:T(8,128)}, u32[]{:S(2)}, u32[]{:S(2)}) collective-permute-start(f32[2048,512]{1,0:T(8,128)} %get-tuple-element.39), channel_id=1, source_target_pairs={{0,1},{1,0},{2,3},{3,2},{4,5},{5,4},{6,7},{7,6}} | collective-permute-start | bytes 12582920 | tf_op jit(solution)/shard_map/ppermute | solution.py:453
  253.6 7.6 %collective-permute-start.1 = (f32[2048,128]{1,0:T(8,128)S(1)}, f32[2048,128]{1,0:T(8,128)}, u32[]{:S(2)}, u32[]{:S(2)}) collective-permute-start(f32[2048,128]{1,0:T(8,128)S(1)} %constant_dynamic-slice_fusion.1), channel_id=1, source_target_pairs={{0,1},{1,0},{2,3},{3,2},{4,5},{5,4},{6,7},{7,6}} | collective-permute-start | bytes 3145736 | tf_op jit(solution)/shard_map/ppermute | solution.py:453
  337.2 110.5 %collective-permute-start.6 = (bf16[4096,2048]{1,0:T(8,128)(2,1)}, bf16[4096,2048]{1,0:T(8,128)(2,1)}, u32[]{:S(2)}, u32[]{:S(2)}) collective-permute-start(bf16[4096,2048]{1,0:T(8,128)(2,1)} %get-tuple-element.47), channel_id=1, source_target_pairs={{0,1},{1,0},{2,3},{3,2},{4,5},{5,4},{6,7},{7,6}} | collective-permute-start | bytes 50331656 | tf_op jit(solution)/shard_map/ppermute | solution.py:453
  337.4 61.1 %collective-permute-start.3 = (f32[512,1024]{1,0:T(8,128)}, f32[512,1024]{1,0:T(8,128)}, u32[]{:S(2)}, u32[]{:S(2)}) collective-permute-start(f32[512,1024]{1,0:T(8,128)} %get-tuple-element.41), channel_id=1, source_target_pairs={{0,4},{4,0},{1,5},{5,1},{2,6},{6,2},{3,7},{7,3}} | collective-permute-start | bytes 6291464 | tf_op jit(solution)/shard_map/ppermute | solution.py:456
  338.9 57.8 %collective-permute-start.5 = (f32[1024,128]{1,0:T(8,128)S(1)}, f32[1024,128]{1,0:T(8,128)S(1)}, u32[]{:S(2)}, u32[]{:S(2)}) collective-permute-start(f32[1024,128]{1,0:T(8,128)S(1)} %constant_dynamic-slice_fusion), channel_id=1, source_target_pairs={{0,4},{4,0},{1,5},{5,1},{2,6},{6,2},{3,7},{7,3}} | collective-permute-start | bytes 1572872 | tf_op jit(solution)/shard_map/ppermute | solution.py:456
  396.8 47.4 %collective-permute-start.4 = (f32[1024,512]{1,0:T(8,128)}, f32[1024,512]{1,0:T(8,128)}, u32[]{:S(2)}, u32[]{:S(2)}) collective-permute-start(f32[1024,512]{1,0:T(8,128)} %get-tuple-element.44), channel_id=1, source_target_pairs={{0,4},{4,0},{1,5},{5,1},{2,6},{6,2},{3,7},{7,3}} | collective-permute-start | bytes 6291464 | tf_op jit(solution)/shard_map/ppermute | solution.py:456
  433.9 64.2 %collective-permute-start.8 = (bf16[2048,2048]{1,0:T(8,128)(2,1)}, bf16[2048,2048]{1,0:T(8,128)(2,1)}, u32[]{:S(2)}, u32[]{:S(2)}) collective-permute-start(bf16[2048,2048]{1,0:T(8,128)(2,1)} %get-tuple-element.53), channel_id=1, source_target_pairs={{0,1},{1,0},{2,3},{3,2},{4,5},{5,4},{6,7},{7,6}} | collective-permute-start | bytes 25165832 | tf_op jit(solution)/shard_map/ppermute | solution.py:453
  483.4 20.6 %collective-permute-start.7 = (bf16[2048,2048]{1,0:T(8,128)(2,1)}, bf16[2048,2048]{1,0:T(8,128)(2,1)}, u32[]{:S(2)}, u32[]{:S(2)}) collective-permute-start(bf16[2048,2048]{1,0:T(8,128)(2,1)} %get-tuple-element.59), channel_id=1, source_target_pairs={{0,1},{1,0},{2,3},{3,2},{4,5},{5,4},{6,7},{7,6}} | collective-permute-start | bytes 25165832 | tf_op jit(solution)/shard_map/ppermute | solution.py:453
  483.4 13.7 %collective-permute-start.9 = (bf16[1024,128]{1,0:T(8,128)(2,1)S(1)}, bf16[1024,128]{1,0:T(8,128)(2,1)S(1)}, u32[]{:S(2)}, u32[]{:S(2)}) collective-permute-start(bf16[1024,128]{1,0:T(8,128)(2,1)S(1)} %add_convert_fusion.2), channel_id=1, source_target_pairs={{0,1},{1,0},{2,3},{3,2},{4,5},{5,4},{6,7},{7,6}} | collective-permute-start | bytes 786440 | tf_op jit(solution)/shard_map/ppermute | solution.py:453

commit v3 on v2

--- a/solution.py
+++ b/solution.py
@@ -195,13 +195,14 @@
     k_fwd.wait_send()
 
 
-def attend_kernel(heads, head_dim, qkv_ref, do_ref, pos_c_ref, pos_r_ref, o_ref, dqkv_ref, seen, pt, dst):
+def attend_kernel(heads, head_dim, qkv_ref, do_ref, pos_ref, o_ref, dqkv_ref, seen, pt, dst):
     seq, width = do_ref.shape
     q_ref, dq_ref = qkv_ref, dqkv_ref
 
     @pl.when(pl.program_id(0) == 0)
     def _():
-        seen[...] = jnp.where(pos_c_ref[...] <= pos_r_ref[...], 1.0, -1.0)
+        query_pos = jnp.broadcast_to(pos_ref[...].astype(F32), (seq, seq))
+        seen[...] = jnp.where(query_pos.T <= query_pos, 1.0, -1.0)
 
     k, v = qkv_ref[:, width : width + head_dim], qkv_ref[:, width + head_dim :]
     kt, vt = k.T, v.T
@@ -251,13 +252,13 @@
     return pl.pallas_call(
         functools.partial(attend_kernel, heads, head_dim),
         grid=(rows // seq,),
-        in_specs=[wider, wide, pl.BlockSpec((seq, 1), lambda i: (0, 0)), pl.BlockSpec((1, seq), lambda i: (0, 0))],
+        in_specs=[wider, wide, pl.BlockSpec((1, seq), lambda i: (0, 0))],
         out_specs=[wide, wider],
         out_shape=[jax.ShapeDtypeStruct((rows, width), BF16), jax.ShapeDtypeStruct((rows, total), BF16)],
         scratch_shapes=[pltpu.VMEM((seq, seq), F32), pltpu.VMEM((seq, heads * seq), BF16), pltpu.VMEM((seq, heads * seq), BF16)],
         cost_estimate=pl.CostEstimate(flops=12 * rows * seq * width, bytes_accessed=8 * rows * width, transcendentals=rows * seq * heads),
         compiler_params=pltpu.CompilerParams(vmem_limit_bytes=LIMIT),
-    )(proj, grad_mixed, positions.reshape(seq, 1), positions.reshape(1, seq))
+    )(proj, grad_mixed, positions.reshape(1, seq))
 
 
 def give_kernel(count, off, a, *refs):
@@ -496,16 +497,17 @@
 
         y, y_send = project_out(after(mixed, send_q), wo, core)
         y_got = swap(y_send)
-        grad_w_out = (keep_o + data_o).astype(BF16)
-        dx, dx_send = grad_tok(after(gqkv, y_send, grad_w_out), wcat, gain, tok, means, inv_stds, core, 0)
+        dx, dx_send = grad_tok(after(gqkv, y_send), wcat, gain, tok, means, inv_stds, core, 0)
         dx_got_0 = swap(dx_send)
         kv_cols = (kv_keep + kv_data).astype(BF16)
         kv_other = swap(kv_cols)
+        dx, dx_send, y = grad_tok(after(gqkv, dx_send, kv_cols), wcat, gain, tok, means, inv_stds, core, 1, (dx, y, y_got))
+        dx_got_1 = swap(dx_send)
+        dx = fill(dx, dx_got_0, core, 0)
+        data_o, data_q, kv_other = lax.optimization_barrier((data_o, data_q, kv_other, dx_send))[:3]
+        grad_w_out = (keep_o + data_o).astype(BF16)
         grad_w_query = (keep_q + data_q).astype(BF16)
         grad_w_kv = jnp.where(c == 0, jnp.concatenate([kv_cols, kv_other], axis=1), jnp.concatenate([kv_other, kv_cols], axis=1))
-        dx, dx_send, y = grad_tok(after(gqkv, dx_send, grad_w_query, kv_cols), wcat, gain, tok, means, inv_stds, core, 1, (dx, y, y_got))
-        dx_got_1 = swap(dx_send)
-        dx = fill(dx, dx_got_0, core, 0)
         dx = fill(dx, dx_got_1, core, 1)
         return y, dx, grad_w_query, grad_w_kv, grad_w_out
 

time: 518 us -> 538 us (1.039)
  waiting for transfers between devices: 87.4 us -> 110 us
    ppermute x3, waiting for transfers between devices: 67.6 us -> 92.2 us  [cross(): return lax.ppermute(a, 'data', datas)]
  transfers between devices with their start and end apart: 10 -> 10, of which waited for: 4 -> 5; matrix products, arithmetic and copies ran while one was open for 2% -> 2% of each run, Pallas kernels for 22% -> 21%
where the time goes in v3:
time: 538 us; the launch traced here: 531 us
  Pallas kernels  402 us (75%)
  waiting for transfers between devices  110 us (20%)
  other arithmetic  11.6 us (2%)
    pallas_call x1, Pallas kernels, layer(): pl.pallas_call(functools.partial(front_kernel, half), in_specs=[ANY, ANY,...  147 us
    ppermute x3, waiting for transfers between devices, cross(): return lax.ppermute(a, 'data', datas)  92.2 us
    pallas_call x2, Pallas kernels, grad_tok(): pl.pallas_call(functools.partial(grad_tok_kernel, earlier is not None), g...  67.8 us
    pallas_call x1, Pallas kernels, attend(): pl.pallas_call(functools.partial(attend_kernel, heads, head_dim), grid=(r...  66.5 us
    pallas_call x1, Pallas kernels, project_out(): pl.pallas_call(out_kernel, grid_spec=pltpu.PrefetchScalarGridSpec(num_sca...  42.1 us
    pallas_call x2, Pallas kernels, give(): pl.pallas_call(functools.partial(give_kernel, len(bs)), grid_spec=pltpu.P...  34.8 us
    pallas_call x2, Pallas kernels, keep(): pl.pallas_call(functools.partial(keep_kernel, half), grid_spec=pltpu.Pref...  32.3 us
    ppermute x7, waiting for transfers between devices, swap(): return lax.ppermute(a, 'model', cores)  17.9 us
  transfers between devices with their start and end apart: 10, of which 5 were waited for; matrix products, arithmetic and copies ran while one was open for 2% of the time, Pallas kernels for 21%

profile of v3, /device:TPU:0, one launch (start us, length us, event | category | flops | bytes accessed | tf_op | source)
XLA Modules:
  0.0 531.1 jit_solution(18273790353444100841)
XLA Ops:
  0.7 0.6 pad_add_fusion.2.off
  1.2 146.8 %shard_map.110 = (bf16[2048,2304]{1,0:T(8,128)(2,1)}, bf16[2048,2048]{1,0:T(8,128)(2,1)}, bf16[4096,2048]{1,0:T(8,128)(2,1)}, f32[4096,128]{1,0:T(8,128)}, f32[4...) custom-call(bf16[8192,2048]{1,0:T(8,128)(2,1)} %tok.5, bf16[8192,2048]{1,0:T(8,128)(2,1)} %b.1, ...), custom_call_target="tpu_custom_call" | custom-call | tf_op jit(solution)/shard_map/pallas_call | solution.py:460
  148.1 66.5 %shard_map.111 = (bf16[4096,2048]{1,0:T(8,128)(2,1)}, bf16[4096,2304]{1,0:T(8,128)(2,1)}) custom-call(bf16[4096,2304]{1,0:T(8,128)(2,1)} %get-tuple-element.36.qkv_ref, bf16[4096,2048]{1,0:T(8,128)(2,1)} %get-tuple-element.37.do_ref, s32[1,256]{1,0:T(1,128)} %bitcast.9), custom_call_target="tpu_custom_call" | custom-call | flops 25769803776 | bytes 67108864 | tf_op jit(solution)/shard_map/pallas_call | solution.py:252
  214.6 14.9 %shard_map.112 = f32[512,2048]{1,0:T(8,128)} custom-call(s32[3]{0:T(128)} %pad_add_fusion.2.off, bf16[4096,2048]{1,0:T(8,128)(2,1)} %get-tuple-element.48.a, bf16[8192,2048]{1,0:T(8,128)(2,1)} %b.1), custom_call_target="tpu_custom_call" | custom-call | flops 8589934592 | bytes 20971520 | tf_op jit(solution)/shard_map/pallas_call | solution.py:276
  229.4 0.4 collective-permute-start
  229.9 0.7 fusion.1
  230.6 19.9 %shard_map.113 = (f32[2048,512]{1,0:T(8,128)}, f32[2048,256]{1,0:T(8,128)}) custom-call(s32[4]{0:T(128)} %get-tuple-element.67.off, bf16[4096,2048]{1,0:T(8,128)(2,1)} %get-tuple-element.46.a, bf16[4096,2304]{1,0:T(8,128)(2,1)} %get-tuple-element.56.refs_0_.refs_1_.b.gqkv, bf16[4096,2304]{1,0:T(8,128)(2,1)} %get-tuple-element.56.refs_0_.refs_1_.b.gqkv), custom_call_target="tpu_custom_call" | custom-call | flops 12884901888 | bytes 23068672 | tf_op jit(solution)/shard_map/pallas_call | solution.py:276
  250.4 0.1 collective-permute-start.2
  250.5 1.3 constant_dynamic-slice_fusion.1
  251.8 0.5 collective-permute-start.1
  252.3 0.6 add_add_fusion.off
  252.9 6.6 %collective-permute-done.1 = f32[2048,128]{1,0:T(8,128)} collective-permute-done((f32[2048,128]{1,0:T(8,128)S(1)}, f32[2048,128]{1,0:T(8,128)}, u32[]{:S(2)}, u32[]{:S(2)}) %collective-permute-start.1) | collective-permute-done | bytes 1048608 | tf_op jit(solution)/shard_map/ppermute | solution.py:454
  259.4 1.6 dynamic-slice_add_fusion
  261.1 0.0 collective-permute-done.got
  261.2 16.3 %shard_map.114 = (f32[512,1024]{1,0:T(8,128)}, f32[512,1024]{1,0:T(8,128)}) custom-call(s32[4]{0:T(128)} %add_add_fusion.off, bf16[4096,2048]{1,0:T(8,128)(2,1)} %get-tuple-element.48.a, bf16[8192,2048]{1,0:T(8,128)(2,1)} %b.1, f32[512,2048]{1,0:T(8,128)} %collective-permute-done.got), custom_call_target="tpu_custom_call" | custom-call | flops 8589934592 | bytes 20971520 | tf_op jit(solution)/shard_map/pallas_call | solution.py:311
  277.4 0.0 collective-permute-done.2.got
  277.4 16.1 %shard_map.115 = (f32[1024,512]{1,0:T(8,128)}, f32[1024,512]{1,0:T(8,128)}) custom-call(s32[4]{0:T(128)} %get-tuple-element.68.off, bf16[4096,2048]{1,0:T(8,128)(2,1)} %get-tuple-element.46.a, bf16[4096,2304]{1,0:T(8,128)(2,1)} %get-tuple-element.56.refs_0_.refs_1_.b.gqkv, f32[2048,512]{1,0:T(8,128)} %collective-permute-done.2.got), custom_call_target="tpu_custom_call" | custom-call | flops 8589934592 | bytes 20971520 | tf_op jit(solution)/shard_map/pallas_call | solution.py:311
  293.5 42.1 %shard_map.116 = (bf16[8192,2048]{1,0:T(8,128)(2,1)}, bf16[4096,2048]{1,0:T(8,128)(2,1)}) custom-call(s32[1]{0:T(128)} %bitcast.off, bf16[4096,2048]{1,0:T(8,128)(2,1)} %get-tuple-element.48.a, bf16[2048,2048]{1,0:T(8,128)(2,1)} %get-tuple-element.49.b), custom_call_target="tpu_custom_call" | custom-call | flops 34359738368 | bytes 50331648 | tf_op jit(solution)/shard_map/pallas_call | solution.py:342
  335.6 0.1 collective-permute-start.4
  335.7 1.5 collective-permute-start.3
  337.2 12.7 %collective-permute-done.3 = f32[1024,128]{1,0:T(8,128)S(1)} collective-permute-done((f32[1024,128]{1,0:T(8,128)S(1)}, f32[1024,128]{1,0:T(8,128)S(1)}, u32[]{:S(2)}, u32[]{:S(2)}) %collective-permute-start.3) | collective-permute-done | bytes 524320 | tf_op jit(solution)/shard_map/ppermute | solution.py:457
  349.9 0.1 add_convert_fusion.2
  350.0 32.1 %shard_map.117 = (bf16[8192,2048]{1,0:T(8,128)(2,1)}, bf16[2048,2048]{1,0:T(8,128)(2,1)}) custom-call(s32[1]{0:T(128)} %bitcast.off, bf16[4096,2304]{1,0:T(8,128)(2,1)} %get-tuple-element.56.refs_0_.refs_1_.b.gqkv, bf16[2048,2304]{1,0:T(8,128)(2,1)} %get-tuple-element.52.wcat, f32[1,2048]{1,0:T(1,128)} %bitcast.7, bf16[8192,2048]{1,0:T(8,128)(2,1)} %tok.5, ...), custom_call_target="tpu_custom_call" | custom-call | flops 19327352832 | bytes 41943040 | tf_op jit(solution)/shard_map/pallas_call | solution.py:398
  382.1 0.0 collective-permute-start.6
  382.1 0.0 collective-permute-done.4.refs_0_
  382.1 35.7 %shard_map.118 = (bf16[8192,2048]{1,0:T(8,128)(2,1)}, bf16[2048,2048]{1,0:T(8,128)(2,1)}, bf16[8192,2048]{1,0:T(8,128)(2,1)}) custom-call(s32[1]{0:T(128)} %bitcast.off, bf16[4096,2304]{1,0:T(8,128)(2,1)} %get-tuple-element.56.refs_0_.refs_1_.b.gqkv, bf16[2048,2304]{1,0:T(8,128)(2,1)} %get-tuple-element.52.wcat, ...), custom_call_target="tpu_custom_call", output_to_operand_aliasing={{0}: (8, {}), {2}: (9, {})} | custom-call | flops 19327352832 | bytes 41943040 | tf_op jit(solution)/shard_map/pallas_call | solution.py:398
  417.8 0.5 collective-permute-start.5
  418.3 1.5 collective-permute-start.8
  419.8 0.5 collective-permute-start.7
  420.3 0.0 collective-permute-start.9
  420.3 11.3 %collective-permute-done.9 = bf16[1024,128]{1,0:T(8,128)(2,1)S(1)} collective-permute-done((bf16[1024,128]{1,0:T(8,128)(2,1)S(1)}, bf16[1024,128]{1,0:T(8,128)(2,1)S(1)}, u32[]{:S(2)}, u32[]{:S(2)}) %collective-permute-start.9) | collective-permute-done | bytes 262176 | tf_op jit(solution)/shard_map/ppermute | solution.py:454
  431.6 35.4 %collective-permute-done.8 = f32[1024,512]{1,0:T(8,128)} collective-permute-done((f32[1024,512]{1,0:T(8,128)}, f32[1024,512]{1,0:T(8,128)}, u32[]{:S(2)}, u32[]{:S(2)}) %collective-permute-start.8) | collective-permute-done | bytes 2097184 | tf_op jit(solution)/shard_map/ppermute | solution.py:457
  467.1 44.0 %collective-permute-done.7 = f32[512,1024]{1,0:T(8,128)} collective-permute-done((f32[512,1024]{1,0:T(8,128)}, f32[512,1024]{1,0:T(8,128)}, u32[]{:S(2)}, u32[]{:S(2)}) %collective-permute-start.7) | collective-permute-done | bytes 2097184 | tf_op jit(solution)/shard_map/ppermute | solution.py:457
  511.1 0.0 collective-permute-done.6.got
  511.1 5.9 %shard_map.119._ = bf16[8192,2048]{1,0:T(8,128)(2,1)} custom-call(s32[1]{0:T(128)} %bitcast.off, bf16[2048,2048]{1,0:T(8,128)(2,1)} %collective-permute-done.6.got, bf16[8192,2048]{1,0:T(8,128)(2,1)} %get-tuple-element.61._), custom_call_target="tpu_custom_call", output_to_operand_aliasing={{}: (2, {})} | custom-call | flops 4194304 | bytes 16777216 | tf_op jit(solution)/shard_map/pallas_call | solution.py:415
  517.0 1.0 maximum_select_fusion
  517.9 3.5 add_convert_fusion
  521.4 3.5 add_convert_fusion.1
  525.0 0.0 collective-permute-done.5.got
  525.0 5.9 %shard_map.120 = bf16[8192,2048]{1,0:T(8,128)(2,1)} custom-call(s32[1]{0:T(128)} %bitcast.off, bf16[2048,2048]{1,0:T(8,128)(2,1)} %collective-permute-done.5.got, bf16[8192,2048]{1,0:T(8,128)(2,1)} %shard_map.119._), custom_call_target="tpu_custom_call", output_to_operand_aliasing={{}: (2, {})} | custom-call | flops 4194304 | bytes 16777216 | tf_op jit(solution)/shard_map/pallas_call | solution.py:415
  (2 shorter events, 0.0 us)
Async XLA Ops:
  229.4 31.7 %collective-permute-start = (f32[512,2048]{1,0:T(8,128)}, f32[512,2048]{1,0:T(8,128)}, u32[]{:S(2)}, u32[]{:S(2)}) collective-permute-start(f32[512,2048]{1,0:T(8,128)} %shard_map.112), channel_id=1, source_target_pairs={{0,1},{1,0},{2,3},{3,2},{4,5},{5,4},{6,7},{7,6}} | collective-permute-start | bytes 12582920 | tf_op jit(solution)/shard_map/ppermute | solution.py:454
  250.4 27.0 %collective-permute-start.2 = (f32[2048,512]{1,0:T(8,128)}, f32[2048,512]{1,0:T(8,128)}, u32[]{:S(2)}, u32[]{:S(2)}) collective-permute-start(f32[2048,512]{1,0:T(8,128)} %get-tuple-element.42), channel_id=1, source_target_pairs={{0,1},{1,0},{2,3},{3,2},{4,5},{5,4},{6,7},{7,6}} | collective-permute-start | bytes 12582920 | tf_op jit(solution)/shard_map/ppermute | solution.py:454
  251.8 7.6 %collective-permute-start.1 = (f32[2048,128]{1,0:T(8,128)S(1)}, f32[2048,128]{1,0:T(8,128)}, u32[]{:S(2)}, u32[]{:S(2)}) collective-permute-start(f32[2048,128]{1,0:T(8,128)S(1)} %constant_dynamic-slice_fusion.1), channel_id=1, source_target_pairs={{0,1},{1,0},{2,3},{3,2},{4,5},{5,4},{6,7},{7,6}} | collective-permute-start | bytes 3145736 | tf_op jit(solution)/shard_map/ppermute | solution.py:454
  335.6 46.5 %collective-permute-start.4 = (bf16[4096,2048]{1,0:T(8,128)(2,1)}, bf16[4096,2048]{1,0:T(8,128)(2,1)}, u32[]{:S(2)}, u32[]{:S(2)}) collective-permute-start(bf16[4096,2048]{1,0:T(8,128)(2,1)} %get-tuple-element.50), channel_id=1, source_target_pairs={{0,1},{1,0},{2,3},{3,2},{4,5},{5,4},{6,7},{7,6}} | collective-permute-start | bytes 50331656 | tf_op jit(solution)/shard_map/ppermute | solution.py:454
  335.7 14.2 %collective-permute-start.3 = (f32[1024,128]{1,0:T(8,128)S(1)}, f32[1024,128]{1,0:T(8,128)S(1)}, u32[]{:S(2)}, u32[]{:S(2)}) collective-permute-start(f32[1024,128]{1,0:T(8,128)S(1)} %constant_dynamic-slice_fusion), channel_id=1, source_target_pairs={{0,4},{4,0},{1,5},{5,1},{2,6},{6,2},{3,7},{7,3}} | collective-permute-start | bytes 1572872 | tf_op jit(solution)/shard_map/ppermute | solution.py:457
  382.1 129.0 %collective-permute-start.6 = (bf16[2048,2048]{1,0:T(8,128)(2,1)}, bf16[2048,2048]{1,0:T(8,128)(2,1)}, u32[]{:S(2)}, u32[]{:S(2)}) collective-permute-start(bf16[2048,2048]{1,0:T(8,128)(2,1)} %get-tuple-element.55), channel_id=1, source_target_pairs={{0,1},{1,0},{2,3},{3,2},{4,5},{5,4},{6,7},{7,6}} | collective-permute-start | bytes 25165832 | tf_op jit(solution)/shard_map/ppermute | solution.py:454
  417.8 107.2 %collective-permute-start.5 = (bf16[2048,2048]{1,0:T(8,128)(2,1)}, bf16[2048,2048]{1,0:T(8,128)(2,1)}, u32[]{:S(2)}, u32[]{:S(2)}) collective-permute-start(bf16[2048,2048]{1,0:T(8,128)(2,1)} %get-tuple-element.60), channel_id=1, source_target_pairs={{0,1},{1,0},{2,3},{3,2},{4,5},{5,4},{6,7},{7,6}} | collective-permute-start | bytes 25165832 | tf_op jit(solution)/shard_map/ppermute | solution.py:454
  418.3 48.8 %collective-permute-start.8 = (f32[1024,512]{1,0:T(8,128)}, f32[1024,512]{1,0:T(8,128)}, u32[]{:S(2)}, u32[]{:S(2)}) collective-permute-start(f32[1024,512]{1,0:T(8,128)} %get-tuple-element.47), channel_id=1, source_target_pairs={{0,4},{4,0},{1,5},{5,1},{2,6},{6,2},{3,7},{7,3}} | collective-permute-start | bytes 6291464 | tf_op jit(solution)/shard_map/ppermute | solution.py:457
  419.8 91.3 %collective-permute-start.7 = (f32[512,1024]{1,0:T(8,128)}, f32[512,1024]{1,0:T(8,128)}, u32[]{:S(2)}, u32[]{:S(2)}) collective-permute-start(f32[512,1024]{1,0:T(8,128)} %get-tuple-element.44), channel_id=1, source_target_pairs={{0,4},{4,0},{1,5},{5,1},{2,6},{6,2},{3,7},{7,3}} | collective-permute-start | bytes 6291464 | tf_op jit(solution)/shard_map/ppermute | solution.py:457
  420.3 11.3 %collective-permute-start.9 = (bf16[1024,128]{1,0:T(8,128)(2,1)S(1)}, bf16[1024,128]{1,0:T(8,128)(2,1)S(1)}, u32[]{:S(2)}, u32[]{:S(2)}) collective-permute-start(bf16[1024,128]{1,0:T(8,128)(2,1)S(1)} %add_convert_fusion.2), channel_id=1, source_target_pairs={{0,1},{1,0},{2,3},{3,2},{4,5},{5,4},{6,7},{7,6}} | collective-permute-start | bytes 786440 | tf_op jit(solution)/shard_map/ppermute | solution.py:454

commit v4 on v3

--- a/solution.py
+++ b/solution.py
@@ -110,7 +110,7 @@
     return pl.ds(m * rows + part * (rows // 2), rows // 2), pl.ds(pl.multiple_of(d * cols, cols), cols)
 
 
-def front_kernel(half, tok, grad, wq, wkv, wo, gain, wcat, wo_full, hidden, means, inv_stds, proj, grad_mixed, wbuf, obuf, kbuf, q_send, q_recv, o_send, o_recv, kv_send, kv_recv, local):
+def front_kernel(half, tok, grad, wq, wkv, wo, gain, wcat, wo_full, hidden, means, inv_stds, proj, grad_mixed, wbuf, kbuf, q_send, q_recv, o_send, o_recv, kv_send, kv_recv, local):
     d, _, x, c, yn, xn, pn = place()
     rows, cols = wq.shape
     depth, width = wo_full.shape[1], wo_full.shape[0]
@@ -131,8 +131,6 @@
     load_q0 = pltpu.make_async_copy(wcat.at[:, mine()], wbuf.at[0], local.at[3])
     load_q1 = pltpu.make_async_copy(wcat.at[:, other()], wbuf.at[1], local.at[4])
     load_kv = pltpu.make_async_copy(wcat.at[:, pl.ds(width, pair)], kbuf, local.at[5])
-    load_o0 = pltpu.make_async_copy(wo_full.at[mine(), :], obuf.at[0], local.at[6])
-    load_o1 = pltpu.make_async_copy(wo_full.at[other(), :], obuf.at[1], local.at[7])
 
     def norm_block(tok_blk, hid_blk, mean_blk, inv_blk):
         rows_f = tok_blk[...].astype(F32)
@@ -153,15 +151,15 @@
 
     big = 1024
 
-    def run(src, weight, dims, out):
+    def run(src, weight, out, lo=0, n=half // big):
         def block(a, o):
-            o[...] = dot(a[...], weight[...], dims).astype(BF16)
+            o[...] = dot(a[...], weight[...], NN).astype(BF16)
 
         pltpu.emit_pipeline(
             block,
-            grid=(half // big,),
-            in_specs=[pl.BlockSpec((big, depth), lambda i: (i, 0))],
-            out_specs=[pl.BlockSpec((big, out.shape[1]), lambda i: (i, 0))],
+            grid=(n,),
+            in_specs=[pl.BlockSpec((big, depth), lambda i: (lo + i, 0))],
+            out_specs=[pl.BlockSpec((big, out.shape[1]), lambda i: (lo + i, 0))],
         )(src, out)
 
     k_out.wait_recv()
@@ -170,27 +168,31 @@
     k_fwd.wait_recv()
     load_kv.start()
     load_kv.wait()
-    run(hidden, kbuf, NN, proj.at[:, pl.ds(width, pair)])
+    run(hidden, kbuf, proj.at[:, pl.ds(width, pair)])
     gather_q.middle()
     gather_o.start()
     gather_q.own_half()
     load_q0.start()
     load_q0.wait()
-    run(hidden, wbuf.at[0], NN, proj.at[:, mine()])
+    run(hidden, wbuf.at[0], proj.at[:, mine()])
     gather_q.finish()
     load_q1.start()
     load_q1.wait()
-    run(hidden, wbuf.at[1], NN, proj.at[:, other()])
+    run(hidden, wbuf.at[1], proj.at[:, other()], 0, half // big // 2)
     gather_o.middle()
+    run(hidden, wbuf.at[1], proj.at[:, other()], half // big // 2, half // big // 2)
     gather_o.own_half()
-    load_o0.start()
-    load_o0.wait()
-    own_grad = grad.at[pl.ds(c * half, half), :]
-    run(own_grad, obuf.at[0], NT, grad_mixed.at[:, mine()])
     gather_o.finish()
-    load_o1.start()
-    load_o1.wait()
-    run(own_grad, obuf.at[1], NT, grad_mixed.at[:, other()])
+
+    def grad_block(a, b, o):
+        o[...] = dot(a[...], b[...], NT).astype(BF16)
+
+    pltpu.emit_pipeline(
+        grad_block,
+        grid=(width // part, half // big),
+        in_specs=[pl.BlockSpec((big, depth), lambda j, i: (i, 0)), pl.BlockSpec((part, depth), lambda j, i: (j, 0))],
+        out_specs=[pl.BlockSpec((big, part), lambda j, i: (i, j))],
+    )(grad.at[pl.ds(c * half, half), :], wo_full, grad_mixed)
     k_out.wait_send()
     k_fwd.wait_send()
 
@@ -470,8 +472,8 @@
                 jax.ShapeDtypeStruct((half, width + pair), BF16),
                 jax.ShapeDtypeStruct((half, width), BF16),
             ],
-            scratch_shapes=[pltpu.VMEM((2, depth, width // 2), BF16), pltpu.VMEM((2, width // 2, depth), BF16), pltpu.VMEM((depth, pair), BF16)]
-            + [sems(9), sems(9), sems(9), sems(9), sems(2), sems(2), sems(8)],
+            scratch_shapes=[pltpu.VMEM((2, depth, width // 2), BF16), pltpu.VMEM((depth, pair), BF16)]
+            + [sems(9), sems(9), sems(9), sems(9), sems(2), sems(2), sems(6)],
             compiler_params=pltpu.CompilerParams(collective_id=0, has_side_effects=True, vmem_limit_bytes=LIMIT),
         )(tok, grad, wq_blk, wkv_blk, wo_blk, gain)
 

time: 538 us -> 534 us (level)
    pallas_call x1, Pallas kernels: 147 us -> 141 us  [layer(): pl.pallas_call(functools.partial(front_kernel, half), in_specs=[ANY, ANY,...]
where the time goes in v4:
time: 534 us; the launch traced here: 526 us
  Pallas kernels  397 us (74%)
  waiting for transfers between devices  111 us (21%)
  other arithmetic  11.6 us (2%)
    pallas_call x1, Pallas kernels, layer(): pl.pallas_call(functools.partial(front_kernel, half), in_specs=[ANY, ANY,...  141 us
    ppermute x3, waiting for transfers between devices, cross(): return lax.ppermute(a, 'data', datas)  93.1 us
    pallas_call x2, Pallas kernels, grad_tok(): pl.pallas_call(functools.partial(grad_tok_kernel, earlier is not None), g...  67.8 us
    pallas_call x1, Pallas kernels, attend(): pl.pallas_call(functools.partial(attend_kernel, heads, head_dim), grid=(r...  67 us
    pallas_call x1, Pallas kernels, project_out(): pl.pallas_call(out_kernel, grid_spec=pltpu.PrefetchScalarGridSpec(num_sca...  42.1 us
    pallas_call x2, Pallas kernels, give(): pl.pallas_call(functools.partial(give_kernel, len(bs)), grid_spec=pltpu.P...  34.8 us
    pallas_call x2, Pallas kernels, keep(): pl.pallas_call(functools.partial(keep_kernel, half), grid_spec=pltpu.Pref...  32.3 us
    ppermute x7, waiting for transfers between devices, swap(): return lax.ppermute(a, 'model', cores)  17.9 us
  transfers between devices with their start and end apart: 10, of which 5 were waited for; matrix products, arithmetic and copies ran while one was open for 2% of the time, Pallas kernels for 21%

profile of v4, /device:TPU:0, one launch (start us, length us, event | category | flops | bytes accessed | tf_op | source)
XLA Modules:
  0.0 525.8 jit_solution(7214698633495291878)
XLA Ops:
  0.7 0.6 pad_add_fusion.2.off
  1.2 141.1 %shard_map.110 = (bf16[2048,2304]{1,0:T(8,128)(2,1)}, bf16[2048,2048]{1,0:T(8,128)(2,1)}, bf16[4096,2048]{1,0:T(8,128)(2,1)}, f32[4096,128]{1,0:T(8,128)}, f32[4...) custom-call(bf16[8192,2048]{1,0:T(8,128)(2,1)} %tok.5, bf16[8192,2048]{1,0:T(8,128)(2,1)} %b.1, ...), custom_call_target="tpu_custom_call" | custom-call | tf_op jit(solution)/shard_map/pallas_call | solution.py:462
  142.4 67.0 %shard_map.111 = (bf16[4096,2048]{1,0:T(8,128)(2,1)}, bf16[4096,2304]{1,0:T(8,128)(2,1)}) custom-call(bf16[4096,2304]{1,0:T(8,128)(2,1)} %get-tuple-element.36.qkv_ref, bf16[4096,2048]{1,0:T(8,128)(2,1)} %get-tuple-element.37.do_ref, s32[1,256]{1,0:T(1,128)} %bitcast.9), custom_call_target="tpu_custom_call" | custom-call | flops 25769803776 | bytes 67108864 | tf_op jit(solution)/shard_map/pallas_call | solution.py:254
  209.3 14.9 %shard_map.112 = f32[512,2048]{1,0:T(8,128)} custom-call(s32[3]{0:T(128)} %pad_add_fusion.2.off, bf16[4096,2048]{1,0:T(8,128)(2,1)} %get-tuple-element.48.a, bf16[8192,2048]{1,0:T(8,128)(2,1)} %b.1), custom_call_target="tpu_custom_call" | custom-call | flops 8589934592 | bytes 20971520 | tf_op jit(solution)/shard_map/pallas_call | solution.py:278
  224.2 0.5 collective-permute-start
  224.7 0.7 fusion.1
  225.3 19.9 %shard_map.113 = (f32[2048,512]{1,0:T(8,128)}, f32[2048,256]{1,0:T(8,128)}) custom-call(s32[4]{0:T(128)} %get-tuple-element.67.off, bf16[4096,2048]{1,0:T(8,128)(2,1)} %get-tuple-element.46.a, bf16[4096,2304]{1,0:T(8,128)(2,1)} %get-tuple-element.56.refs_0_.refs_1_.b.gqkv, bf16[4096,2304]{1,0:T(8,128)(2,1)} %get-tuple-element.56.refs_0_.refs_1_.b.gqkv), custom_call_target="tpu_custom_call" | custom-call | flops 12884901888 | bytes 23068672 | tf_op jit(solution)/shard_map/pallas_call | solution.py:278
  245.2 0.0 collective-permute-start.2
  245.3 1.3 constant_dynamic-slice_fusion.1
  246.6 0.5 collective-permute-start.1
  247.0 0.6 add_add_fusion.off
  247.6 6.6 %collective-permute-done.1 = f32[2048,128]{1,0:T(8,128)} collective-permute-done((f32[2048,128]{1,0:T(8,128)S(1)}, f32[2048,128]{1,0:T(8,128)}, u32[]{:S(2)}, u32[]{:S(2)}) %collective-permute-start.1) | collective-permute-done | bytes 1048608 | tf_op jit(solution)/shard_map/ppermute | solution.py:456
  254.2 1.6 dynamic-slice_add_fusion
  255.9 0.0 collective-permute-done.got
  255.9 16.1 %shard_map.114 = (f32[512,1024]{1,0:T(8,128)}, f32[512,1024]{1,0:T(8,128)}) custom-call(s32[4]{0:T(128)} %add_add_fusion.off, bf16[4096,2048]{1,0:T(8,128)(2,1)} %get-tuple-element.48.a, bf16[8192,2048]{1,0:T(8,128)(2,1)} %b.1, f32[512,2048]{1,0:T(8,128)} %collective-permute-done.got), custom_call_target="tpu_custom_call" | custom-call | flops 8589934592 | bytes 20971520 | tf_op jit(solution)/shard_map/pallas_call | solution.py:313
  272.0 0.0 collective-permute-done.2.got
  272.0 16.2 %shard_map.115 = (f32[1024,512]{1,0:T(8,128)}, f32[1024,512]{1,0:T(8,128)}) custom-call(s32[4]{0:T(128)} %get-tuple-element.68.off, bf16[4096,2048]{1,0:T(8,128)(2,1)} %get-tuple-element.46.a, bf16[4096,2304]{1,0:T(8,128)(2,1)} %get-tuple-element.56.refs_0_.refs_1_.b.gqkv, f32[2048,512]{1,0:T(8,128)} %collective-permute-done.2.got), custom_call_target="tpu_custom_call" | custom-call | flops 8589934592 | bytes 20971520 | tf_op jit(solution)/shard_map/pallas_call | solution.py:313
  288.3 42.1 %shard_map.116 = (bf16[8192,2048]{1,0:T(8,128)(2,1)}, bf16[4096,2048]{1,0:T(8,128)(2,1)}) custom-call(s32[1]{0:T(128)} %bitcast.off, bf16[4096,2048]{1,0:T(8,128)(2,1)} %get-tuple-element.48.a, bf16[2048,2048]{1,0:T(8,128)(2,1)} %get-tuple-element.49.b), custom_call_target="tpu_custom_call" | custom-call | flops 34359738368 | bytes 50331648 | tf_op jit(solution)/shard_map/pallas_call | solution.py:344
  330.4 0.1 collective-permute-start.4
  330.5 0.5 collective-permute-start.3
  331.0 13.7 %collective-permute-done.3 = f32[1024,128]{1,0:T(8,128)S(1)} collective-permute-done((f32[1024,128]{1,0:T(8,128)S(1)}, f32[1024,128]{1,0:T(8,128)S(1)}, u32[]{:S(2)}, u32[]{:S(2)}) %collective-permute-start.3) | collective-permute-done | bytes 524320 | tf_op jit(solution)/shard_map/ppermute | solution.py:459
  344.7 0.1 add_convert_fusion.2
  344.8 32.1 %shard_map.117 = (bf16[8192,2048]{1,0:T(8,128)(2,1)}, bf16[2048,2048]{1,0:T(8,128)(2,1)}) custom-call(s32[1]{0:T(128)} %bitcast.off, bf16[4096,2304]{1,0:T(8,128)(2,1)} %get-tuple-element.56.refs_0_.refs_1_.b.gqkv, bf16[2048,2304]{1,0:T(8,128)(2,1)} %get-tuple-element.52.wcat, f32[1,2048]{1,0:T(1,128)} %bitcast.7, bf16[8192,2048]{1,0:T(8,128)(2,1)} %tok.5, ...), custom_call_target="tpu_custom_call" | custom-call | flops 19327352832 | bytes 41943040 | tf_op jit(solution)/shard_map/pallas_call | solution.py:400
  376.8 0.0 collective-permute-start.6
  376.8 0.0 collective-permute-done.4.refs_0_
  376.8 35.7 %shard_map.118 = (bf16[8192,2048]{1,0:T(8,128)(2,1)}, bf16[2048,2048]{1,0:T(8,128)(2,1)}, bf16[8192,2048]{1,0:T(8,128)(2,1)}) custom-call(s32[1]{0:T(128)} %bitcast.off, bf16[4096,2304]{1,0:T(8,128)(2,1)} %get-tuple-element.56.refs_0_.refs_1_.b.gqkv, bf16[2048,2304]{1,0:T(8,128)(2,1)} %get-tuple-element.52.wcat, ...), custom_call_target="tpu_custom_call", output_to_operand_aliasing={{0}: (8, {}), {2}: (9, {})} | custom-call | flops 19327352832 | bytes 41943040 | tf_op jit(solution)/shard_map/pallas_call | solution.py:400
  412.6 0.5 collective-permute-start.5
  413.0 0.5 collective-permute-start.8
  413.6 1.5 collective-permute-start.7
  415.1 0.0 collective-permute-start.9
  415.1 11.3 %collective-permute-done.9 = bf16[1024,128]{1,0:T(8,128)(2,1)S(1)} collective-permute-done((bf16[1024,128]{1,0:T(8,128)(2,1)S(1)}, bf16[1024,128]{1,0:T(8,128)(2,1)S(1)}, u32[]{:S(2)}, u32[]{:S(2)}) %collective-permute-start.9) | collective-permute-done | bytes 262176 | tf_op jit(solution)/shard_map/ppermute | solution.py:456
  426.4 35.4 %collective-permute-done.8 = f32[1024,512]{1,0:T(8,128)} collective-permute-done((f32[1024,512]{1,0:T(8,128)}, f32[1024,512]{1,0:T(8,128)}, u32[]{:S(2)}, u32[]{:S(2)}) %collective-permute-start.8) | collective-permute-done | bytes 2097184 | tf_op jit(solution)/shard_map/ppermute | solution.py:459
  461.9 44.0 %collective-permute-done.7 = f32[512,1024]{1,0:T(8,128)} collective-permute-done((f32[512,1024]{1,0:T(8,128)}, f32[512,1024]{1,0:T(8,128)}, u32[]{:S(2)}, u32[]{:S(2)}) %collective-permute-start.7) | collective-permute-done | bytes 2097184 | tf_op jit(solution)/shard_map/ppermute | solution.py:459
  505.9 0.0 collective-permute-done.6.got
  505.9 5.9 %shard_map.119._ = bf16[8192,2048]{1,0:T(8,128)(2,1)} custom-call(s32[1]{0:T(128)} %bitcast.off, bf16[2048,2048]{1,0:T(8,128)(2,1)} %collective-permute-done.6.got, bf16[8192,2048]{1,0:T(8,128)(2,1)} %get-tuple-element.61._), custom_call_target="tpu_custom_call", output_to_operand_aliasing={{}: (2, {})} | custom-call | flops 4194304 | bytes 16777216 | tf_op jit(solution)/shard_map/pallas_call | solution.py:417
  511.7 1.0 maximum_select_fusion
  512.7 3.5 add_convert_fusion
  516.2 3.5 add_convert_fusion.1
  519.7 0.0 collective-permute-done.5.got
  519.7 5.9 %shard_map.120 = bf16[8192,2048]{1,0:T(8,128)(2,1)} custom-call(s32[1]{0:T(128)} %bitcast.off, bf16[2048,2048]{1,0:T(8,128)(2,1)} %collective-permute-done.5.got, bf16[8192,2048]{1,0:T(8,128)(2,1)} %shard_map.119._), custom_call_target="tpu_custom_call", output_to_operand_aliasing={{}: (2, {})} | custom-call | flops 4194304 | bytes 16777216 | tf_op jit(solution)/shard_map/pallas_call | solution.py:417
  (2 shorter events, 0.0 us)
Async XLA Ops:
  224.2 31.7 %collective-permute-start = (f32[512,2048]{1,0:T(8,128)}, f32[512,2048]{1,0:T(8,128)}, u32[]{:S(2)}, u32[]{:S(2)}) collective-permute-start(f32[512,2048]{1,0:T(8,128)} %shard_map.112), channel_id=1, source_target_pairs={{0,1},{1,0},{2,3},{3,2},{4,5},{5,4},{6,7},{7,6}} | collective-permute-start | bytes 12582920 | tf_op jit(solution)/shard_map/ppermute | solution.py:456
  245.2 26.8 %collective-permute-start.2 = (f32[2048,512]{1,0:T(8,128)}, f32[2048,512]{1,0:T(8,128)}, u32[]{:S(2)}, u32[]{:S(2)}) collective-permute-start(f32[2048,512]{1,0:T(8,128)} %get-tuple-element.42), channel_id=1, source_target_pairs={{0,1},{1,0},{2,3},{3,2},{4,5},{5,4},{6,7},{7,6}} | collective-permute-start | bytes 12582920 | tf_op jit(solution)/shard_map/ppermute | solution.py:456
  246.6 7.7 %collective-permute-start.1 = (f32[2048,128]{1,0:T(8,128)S(1)}, f32[2048,128]{1,0:T(8,128)}, u32[]{:S(2)}, u32[]{:S(2)}) collective-permute-start(f32[2048,128]{1,0:T(8,128)S(1)} %constant_dynamic-slice_fusion.1), channel_id=1, source_target_pairs={{0,1},{1,0},{2,3},{3,2},{4,5},{5,4},{6,7},{7,6}} | collective-permute-start | bytes 3145736 | tf_op jit(solution)/shard_map/ppermute | solution.py:456
  330.4 46.5 %collective-permute-start.4 = (bf16[4096,2048]{1,0:T(8,128)(2,1)}, bf16[4096,2048]{1,0:T(8,128)(2,1)}, u32[]{:S(2)}, u32[]{:S(2)}) collective-permute-start(bf16[4096,2048]{1,0:T(8,128)(2,1)} %get-tuple-element.50), channel_id=1, source_target_pairs={{0,1},{1,0},{2,3},{3,2},{4,5},{5,4},{6,7},{7,6}} | collective-permute-start | bytes 50331656 | tf_op jit(solution)/shard_map/ppermute | solution.py:456
  330.5 14.2 %collective-permute-start.3 = (f32[1024,128]{1,0:T(8,128)S(1)}, f32[1024,128]{1,0:T(8,128)S(1)}, u32[]{:S(2)}, u32[]{:S(2)}) collective-permute-start(f32[1024,128]{1,0:T(8,128)S(1)} %constant_dynamic-slice_fusion), channel_id=1, source_target_pairs={{0,4},{4,0},{1,5},{5,1},{2,6},{6,2},{3,7},{7,3}} | collective-permute-start | bytes 1572872 | tf_op jit(solution)/shard_map/ppermute | solution.py:459
  376.8 129.0 %collective-permute-start.6 = (bf16[2048,2048]{1,0:T(8,128)(2,1)}, bf16[2048,2048]{1,0:T(8,128)(2,1)}, u32[]{:S(2)}, u32[]{:S(2)}) collective-permute-start(bf16[2048,2048]{1,0:T(8,128)(2,1)} %get-tuple-element.55), channel_id=1, source_target_pairs={{0,1},{1,0},{2,3},{3,2},{4,5},{5,4},{6,7},{7,6}} | collective-permute-start | bytes 25165832 | tf_op jit(solution)/shard_map/ppermute | solution.py:456
  412.6 107.2 %collective-permute-start.5 = (bf16[2048,2048]{1,0:T(8,128)(2,1)}, bf16[2048,2048]{1,0:T(8,128)(2,1)}, u32[]{:S(2)}, u32[]{:S(2)}) collective-permute-start(bf16[2048,2048]{1,0:T(8,128)(2,1)} %get-tuple-element.60), channel_id=1, source_target_pairs={{0,1},{1,0},{2,3},{3,2},{4,5},{5,4},{6,7},{7,6}} | collective-permute-start | bytes 25165832 | tf_op jit(solution)/shard_map/ppermute | solution.py:456
  413.0 48.8 %collective-permute-start.8 = (f32[1024,512]{1,0:T(8,128)}, f32[1024,512]{1,0:T(8,128)}, u32[]{:S(2)}, u32[]{:S(2)}) collective-permute-start(f32[1024,512]{1,0:T(8,128)} %get-tuple-element.47), channel_id=1, source_target_pairs={{0,4},{4,0},{1,5},{5,1},{2,6},{6,2},{3,7},{7,3}} | collective-permute-start | bytes 6291464 | tf_op jit(solution)/shard_map/ppermute | solution.py:459
  413.6 92.3 %collective-permute-start.7 = (f32[512,1024]{1,0:T(8,128)}, f32[512,1024]{1,0:T(8,128)}, u32[]{:S(2)}, u32[]{:S(2)}) collective-permute-start(f32[512,1024]{1,0:T(8,128)} %get-tuple-element.44), channel_id=1, source_target_pairs={{0,4},{4,0},{1,5},{5,1},{2,6},{6,2},{3,7},{7,3}} | collective-permute-start | bytes 6291464 | tf_op jit(solution)/shard_map/ppermute | solution.py:459
  415.1 11.3 %collective-permute-start.9 = (bf16[1024,128]{1,0:T(8,128)(2,1)S(1)}, bf16[1024,128]{1,0:T(8,128)(2,1)S(1)}, u32[]{:S(2)}, u32[]{:S(2)}) collective-permute-start(bf16[1024,128]{1,0:T(8,128)(2,1)S(1)} %add_convert_fusion.2), channel_id=1, source_target_pairs={{0,1},{1,0},{2,3},{3,2},{4,5},{5,4},{6,7},{7,6}} | collective-permute-start | bytes 786440 | tf_op jit(solution)/shard_map/ppermute | solution.py:456

commit v5 on v4

--- a/solution.py
+++ b/solution.py
@@ -331,28 +331,44 @@
     )(offs, a, b, got)
 
 
-def out_kernel(off, a, b, full, send):
+def out_kernel(passing, off, a, b, *refs):
+    if passing:
+        got, _, _, full, send, dx_full = refs
+        dx_full[...] = got[...]
+    else:
+        full, send = refs
     block = dot(a[...], b[...], NN).astype(BF16)
     full[...] = block
     send[...] = block
 
 
-def project_out(mixed, wo, core, tile=1024):
+def project_out(mixed, wo, core, part, earlier=None, tile=1024):
     rows, depth = mixed.shape
     width = wo.shape[1]
     blocks = rows // tile
+    steps = blocks // 2
+    first = part * steps
+    in_specs = [pl.BlockSpec((tile, depth), lambda j, i, off: (first + i, 0)), pl.BlockSpec((depth, tile), lambda j, i, off: (0, j))]
+    out_specs = [pl.BlockSpec((tile, tile), lambda j, i, off: (off[0] * blocks + first + i, j)), pl.BlockSpec((tile, tile), lambda j, i, off: (i, j))]
+    out_shape = [jax.ShapeDtypeStruct((2 * rows, width), BF16), jax.ShapeDtypeStruct((rows // 2, width), BF16)]
+    args, aliases = [core, mixed, wo], {}
+    if earlier is not None:
+        y, dx, got = earlier
+        args += [got, y, dx]
+        turns = steps * (width // tile)
+        wide = rows // turns
+        in_specs += [pl.BlockSpec((wide, width), lambda j, i, off: (j * steps + i, 0)), ANY, ANY]
+        out_specs.append(pl.BlockSpec((wide, width), lambda j, i, off: ((1 - off[0]) * turns + j * steps + i, 0)))
+        out_shape.append(jax.ShapeDtypeStruct(dx.shape, BF16))
+        aliases = {4: 0, 5: 2}
     return pl.pallas_call(
-        out_kernel,
-        grid_spec=pltpu.PrefetchScalarGridSpec(
-            num_scalar_prefetch=1,
-            grid=(width // tile, blocks),
-            in_specs=[pl.BlockSpec((tile, depth), lambda j, i, off: (i, 0)), pl.BlockSpec((depth, tile), lambda j, i, off: (0, j))],
-            out_specs=[pl.BlockSpec((tile, tile), lambda j, i, off: (off[0] * blocks + i, j)), pl.BlockSpec((tile, tile), lambda j, i, off: (i, j))],
-        ),
-        out_shape=[jax.ShapeDtypeStruct((2 * rows, width), BF16), jax.ShapeDtypeStruct((rows, width), BF16)],
-        cost_estimate=pl.CostEstimate(flops=2 * rows * depth * width, bytes_accessed=2 * rows * (depth + 2 * width), transcendentals=0),
+        functools.partial(out_kernel, earlier is not None),
+        grid_spec=pltpu.PrefetchScalarGridSpec(num_scalar_prefetch=1, grid=(width // tile, steps), in_specs=in_specs, out_specs=out_specs),
+        out_shape=out_shape,
+        input_output_aliases=aliases,
+        cost_estimate=pl.CostEstimate(flops=rows * depth * width, bytes_accessed=5 * rows * depth, transcendentals=0),
         compiler_params=pltpu.CompilerParams(vmem_limit_bytes=LIMIT),
-    )(core, mixed, wo)
+    )(*args)
 
 
 def grad_tok_kernel(passing, off, gqkv, wcat, gain, tok, means, inv_stds, *refs):
@@ -369,12 +385,11 @@
     send[...] = block
 
 
-def grad_tok(gqkv, wcat, gain, tok, means, inv_stds, core, part, earlier=None, tile=512):
+def grad_tok(gqkv, wcat, gain, tok, means, inv_stds, core, earlier=None, tile=512):
     rows, total = gqkv.shape
     depth = wcat.shape[0]
     blocks = rows // tile
-    steps = blocks // 2
-    first = part * steps
+    steps, first = blocks, 0
     whole = lambda i, off: (0, 0)
     once = pl.Buffered(1)
     in_specs = [
@@ -387,7 +402,7 @@
     ]
     own = pl.BlockSpec((tile, depth), lambda i, off: (off[0] * blocks + first + i, 0))
     out_specs = [own, pl.BlockSpec((tile, depth), lambda i, off: (i, 0))]
-    out_shape = [jax.ShapeDtypeStruct((2 * rows, depth), BF16), jax.ShapeDtypeStruct((rows // 2, depth), BF16)]
+    out_shape = [jax.ShapeDtypeStruct((2 * rows, depth), BF16), jax.ShapeDtypeStruct((rows, depth), BF16)]
     args, aliases = [core, gqkv, wcat, gain, tok, means, inv_stds], {}
     if earlier is not None:
         dx, y, got = earlier
@@ -497,20 +512,20 @@
         send_q, keep_q = keep(after(hidden, send_o, kv_give), gqkv, index(0, 0, mine, d), (depth, piece), 0, got_q)
         data_q = cross(send_q)
 
-        y, y_send = project_out(after(mixed, send_q), wo, core)
-        y_got = swap(y_send)
-        dx, dx_send = grad_tok(after(gqkv, y_send), wcat, gain, tok, means, inv_stds, core, 0)
-        dx_got_0 = swap(dx_send)
+        dx, dx_send = grad_tok(after(gqkv, send_q), wcat, gain, tok, means, inv_stds, core)
+        dx_got = swap(dx_send)
+        y, y_send = project_out(after(mixed, dx_send), wo, core, 0)
+        y_got_0 = swap(y_send)
         kv_cols = (kv_keep + kv_data).astype(BF16)
         kv_other = swap(kv_cols)
-        dx, dx_send, y = grad_tok(after(gqkv, dx_send, kv_cols), wcat, gain, tok, means, inv_stds, core, 1, (dx, y, y_got))
-        dx_got_1 = swap(dx_send)
-        dx = fill(dx, dx_got_0, core, 0)
-        data_o, data_q, kv_other = lax.optimization_barrier((data_o, data_q, kv_other, dx_send))[:3]
+        y, y_send, dx = project_out(after(mixed, y_send, kv_cols), wo, core, 1, (y, dx, dx_got))
+        y_got_1 = swap(y_send)
+        y = fill(y, y_got_0, core, 0)
+        data_o, data_q, kv_other = lax.optimization_barrier((data_o, data_q, kv_other, y_send))[:3]
         grad_w_out = (keep_o + data_o).astype(BF16)
         grad_w_query = (keep_q + data_q).astype(BF16)
         grad_w_kv = jnp.where(c == 0, jnp.concatenate([kv_cols, kv_other], axis=1), jnp.concatenate([kv_other, kv_cols], axis=1))
-        dx = fill(dx, dx_got_1, core, 1)
+        y = fill(y, y_got_1, core, 1)
         return y, dx, grad_w_query, grad_w_kv, grad_w_out
 
     return jax.shard_map(

time: 534 us -> 529 us (level); the launches traced: 526 us -> 528 us
    pallas_call x1 -> x2, Pallas kernels: 42.1 us -> 56.5 us  [project_out(): pl.pallas_call(functools.partial(out_kernel, earlier is not None), grid_s...]
    pallas_call x2 -> x1, Pallas kernels: 67.8 us -> 56.2 us  [grad_tok(): pl.pallas_call(functools.partial(grad_tok_kernel, earlier is not None), g...]
  transfers between devices with their start and end apart: 10 -> 10, of which waited for: 5 -> 5; matrix products, arithmetic and copies ran while one was open for 2% -> 2% of each run, Pallas kernels for 21% -> 19%
where the time goes in v5:
time: 529 us; the launch traced here: 528 us
  Pallas kernels  399 us (75%)
  waiting for transfers between devices  111 us (21%)
  other arithmetic  11.6 us (2%)
    pallas_call x1, Pallas kernels, layer(): pl.pallas_call(functools.partial(front_kernel, half), in_specs=[ANY, ANY,...  141 us
    ppermute x3, waiting for transfers between devices, cross(): return lax.ppermute(a, 'data', datas)  93.1 us
    pallas_call x1, Pallas kernels, attend(): pl.pallas_call(functools.partial(attend_kernel, heads, head_dim), grid=(r...  66.6 us
    pallas_call x2, Pallas kernels, project_out(): pl.pallas_call(functools.partial(out_kernel, earlier is not None), grid_s...  56.5 us
    pallas_call x1, Pallas kernels, grad_tok(): pl.pallas_call(functools.partial(grad_tok_kernel, earlier is not None), g...  56.2 us
    pallas_call x2, Pallas kernels, give(): pl.pallas_call(functools.partial(give_kernel, len(bs)), grid_spec=pltpu.P...  34.8 us
    pallas_call x2, Pallas kernels, keep(): pl.pallas_call(functools.partial(keep_kernel, half), grid_spec=pltpu.Pref...  32.4 us
    ppermute x7, waiting for transfers between devices, swap(): return lax.ppermute(a, 'model', cores)  17.9 us
  transfers between devices with their start and end apart: 10, of which 5 were waited for; matrix products, arithmetic and copies ran while one was open for 2% of the time, Pallas kernels for 19%

profile of v5, /device:TPU:0, one launch (start us, length us, event | category | flops | bytes accessed | tf_op | source)
XLA Modules:
  0.0 528.0 jit_solution(6326771241285815120)
XLA Ops:
  0.7 0.6 pad_add_fusion.2.off
  1.2 141.1 %shard_map.110 = (bf16[2048,2304]{1,0:T(8,128)(2,1)}, bf16[2048,2048]{1,0:T(8,128)(2,1)}, bf16[4096,2048]{1,0:T(8,128)(2,1)}, f32[4096,128]{1,0:T(8,128)}, f32[4...) custom-call(bf16[8192,2048]{1,0:T(8,128)(2,1)} %tok.3, bf16[8192,2048]{1,0:T(8,128)(2,1)} %b.1, ...), custom_call_target="tpu_custom_call" | custom-call | tf_op jit(solution)/shard_map/pallas_call | solution.py:477
  142.3 66.6 %shard_map.111 = (bf16[4096,2048]{1,0:T(8,128)(2,1)}, bf16[4096,2304]{1,0:T(8,128)(2,1)}) custom-call(bf16[4096,2304]{1,0:T(8,128)(2,1)} %get-tuple-element.36.qkv_ref, bf16[4096,2048]{1,0:T(8,128)(2,1)} %get-tuple-element.37.do_ref, s32[1,256]{1,0:T(1,128)} %bitcast.8), custom_call_target="tpu_custom_call" | custom-call | flops 25769803776 | bytes 67108864 | tf_op jit(solution)/shard_map/pallas_call | solution.py:254
  209.0 14.9 %shard_map.112 = f32[512,2048]{1,0:T(8,128)} custom-call(s32[3]{0:T(128)} %pad_add_fusion.2.off, bf16[4096,2048]{1,0:T(8,128)(2,1)} %get-tuple-element.56.a, bf16[8192,2048]{1,0:T(8,128)(2,1)} %b.1), custom_call_target="tpu_custom_call" | custom-call | flops 8589934592 | bytes 20971520 | tf_op jit(solution)/shard_map/pallas_call | solution.py:278
  223.9 0.4 collective-permute-start
  224.3 0.7 fusion.1
  224.9 19.9 %shard_map.113 = (f32[2048,512]{1,0:T(8,128)}, f32[2048,256]{1,0:T(8,128)}) custom-call(s32[4]{0:T(128)} %get-tuple-element.67.off, bf16[4096,2048]{1,0:T(8,128)(2,1)} %get-tuple-element.46.a, bf16[4096,2304]{1,0:T(8,128)(2,1)} %get-tuple-element.48.refs_0_.refs_1_.b.gqkv, bf16[4096,2304]{1,0:T(8,128)(2,1)} %get-tuple-element.48.refs_0_.refs_1_.b.gqkv), custom_call_target="tpu_custom_call" | custom-call | flops 12884901888 | bytes 23068672 | tf_op jit(solution)/shard_map/pallas_call | solution.py:278
  244.8 0.1 collective-permute-start.2
  244.9 1.3 constant_dynamic-slice_fusion.1
  246.2 0.4 collective-permute-start.1
  246.6 0.6 add_add_fusion.off
  247.2 6.6 %collective-permute-done.1 = f32[2048,128]{1,0:T(8,128)} collective-permute-done((f32[2048,128]{1,0:T(8,128)S(1)}, f32[2048,128]{1,0:T(8,128)}, u32[]{:S(2)}, u32[]{:S(2)}) %collective-permute-start.1) | collective-permute-done | bytes 1048608 | tf_op jit(solution)/shard_map/ppermute | solution.py:471
  253.8 1.6 dynamic-slice_add_fusion
  255.5 0.0 collective-permute-done.got
  255.5 16.1 %shard_map.114 = (f32[512,1024]{1,0:T(8,128)}, f32[512,1024]{1,0:T(8,128)}) custom-call(s32[4]{0:T(128)} %add_add_fusion.off, bf16[4096,2048]{1,0:T(8,128)(2,1)} %get-tuple-element.56.a, bf16[8192,2048]{1,0:T(8,128)(2,1)} %b.1, f32[512,2048]{1,0:T(8,128)} %collective-permute-done.got), custom_call_target="tpu_custom_call" | custom-call | flops 8589934592 | bytes 20971520 | tf_op jit(solution)/shard_map/pallas_call | solution.py:313
  271.6 0.0 collective-permute-done.2.got
  271.6 16.3 %shard_map.115 = (f32[1024,512]{1,0:T(8,128)}, f32[1024,512]{1,0:T(8,128)}) custom-call(s32[4]{0:T(128)} %get-tuple-element.68.off, bf16[4096,2048]{1,0:T(8,128)(2,1)} %get-tuple-element.46.a, bf16[4096,2304]{1,0:T(8,128)(2,1)} %get-tuple-element.48.refs_0_.refs_1_.b.gqkv, f32[2048,512]{1,0:T(8,128)} %collective-permute-done.2.got), custom_call_target="tpu_custom_call" | custom-call | flops 8589934592 | bytes 20971520 | tf_op jit(solution)/shard_map/pallas_call | solution.py:313
  287.9 56.2 %shard_map.116 = (bf16[8192,2048]{1,0:T(8,128)(2,1)}, bf16[4096,2048]{1,0:T(8,128)(2,1)}) custom-call(s32[1]{0:T(128)} %bitcast.off, bf16[4096,2304]{1,0:T(8,128)(2,1)} %get-tuple-element.48.refs_0_.refs_1_.b.gqkv, bf16[2048,2304]{1,0:T(8,128)(2,1)} %get-tuple-element.49.wcat, f32[1,2048]{1,0:T(1,128)} %bitcast.7, bf16[8192,2048]{1,0:T(8,128)(2,1)} %tok.3, ...), custom_call_target="tpu_custom_call" | custom-call | flops 19327352832 | bytes 41943040 | tf_op jit(solution)/shard_map/pallas_call | solution.py:415
  344.1 0.1 collective-permute-start.4
  344.2 0.5 collective-permute-start.3
  344.8 13.7 %collective-permute-done.3 = f32[1024,128]{1,0:T(8,128)S(1)} collective-permute-done((f32[1024,128]{1,0:T(8,128)S(1)}, f32[1024,128]{1,0:T(8,128)S(1)}, u32[]{:S(2)}, u32[]{:S(2)}) %collective-permute-start.3) | collective-permute-done | bytes 524320 | tf_op jit(solution)/shard_map/ppermute | solution.py:474
  358.5 0.1 add_convert_fusion.2
  358.5 24.0 %shard_map.117 = (bf16[8192,2048]{1,0:T(8,128)(2,1)}, bf16[2048,2048]{1,0:T(8,128)(2,1)}) custom-call(s32[1]{0:T(128)} %bitcast.off, bf16[4096,2048]{1,0:T(8,128)(2,1)} %get-tuple-element.56.a, bf16[2048,2048]{1,0:T(8,128)(2,1)} %get-tuple-element.54.b), custom_call_target="tpu_custom_call" | custom-call | flops 17179869184 | bytes 41943040 | tf_op jit(solution)/shard_map/pallas_call | solution.py:364
  382.6 0.0 collective-permute-start.6
  382.6 0.0 collective-permute-done.4.refs_0_
  382.6 32.4 %shard_map.118 = (bf16[8192,2048]{1,0:T(8,128)(2,1)}, bf16[2048,2048]{1,0:T(8,128)(2,1)}, bf16[8192,2048]{1,0:T(8,128)(2,1)}) custom-call(s32[1]{0:T(128)} %bitcast.off, bf16[4096,2048]{1,0:T(8,128)(2,1)} %get-tuple-element.56.a, bf16[2048,2048]{1,0:T(8,128)(2,1)} %get-tuple-element.54.b, ...), custom_call_target="tpu_custom_call", output_to_operand_aliasing={{0}: (4, {}), {2}: (5, {})} | custom-call | flops 17179869184 | bytes 41943040 | tf_op jit(solution)/shard_map/pallas_call | solution.py:364
  415.0 0.5 collective-permute-start.5
  415.5 0.5 collective-permute-start.8
  416.0 1.5 collective-permute-start.7
  417.5 0.0 collective-permute-start.9
  417.5 11.3 %collective-permute-done.9 = bf16[1024,128]{1,0:T(8,128)(2,1)S(1)} collective-permute-done((bf16[1024,128]{1,0:T(8,128)(2,1)S(1)}, bf16[1024,128]{1,0:T(8,128)(2,1)S(1)}, u32[]{:S(2)}, u32[]{:S(2)}) %collective-permute-start.9) | collective-permute-done | bytes 262176 | tf_op jit(solution)/shard_map/ppermute | solution.py:471
  428.8 35.4 %collective-permute-done.8 = f32[1024,512]{1,0:T(8,128)} collective-permute-done((f32[1024,512]{1,0:T(8,128)}, f32[1024,512]{1,0:T(8,128)}, u32[]{:S(2)}, u32[]{:S(2)}) %collective-permute-start.8) | collective-permute-done | bytes 2097184 | tf_op jit(solution)/shard_map/ppermute | solution.py:474
  464.3 44.0 %collective-permute-done.7 = f32[512,1024]{1,0:T(8,128)} collective-permute-done((f32[512,1024]{1,0:T(8,128)}, f32[512,1024]{1,0:T(8,128)}, u32[]{:S(2)}, u32[]{:S(2)}) %collective-permute-start.7) | collective-permute-done | bytes 2097184 | tf_op jit(solution)/shard_map/ppermute | solution.py:474
  508.3 0.0 collective-permute-done.6.got
  508.3 5.9 %shard_map.119._ = bf16[8192,2048]{1,0:T(8,128)(2,1)} custom-call(s32[1]{0:T(128)} %bitcast.off, bf16[2048,2048]{1,0:T(8,128)(2,1)} %collective-permute-done.6.got, bf16[8192,2048]{1,0:T(8,128)(2,1)} %get-tuple-element.60._), custom_call_target="tpu_custom_call", output_to_operand_aliasing={{}: (2, {})} | custom-call | flops 4194304 | bytes 16777216 | tf_op jit(solution)/shard_map/pallas_call | solution.py:432
  514.1 1.0 maximum_select_fusion
  515.1 3.5 add_convert_fusion
  518.6 3.5 add_convert_fusion.1
  522.2 0.0 collective-permute-done.5.got
  522.2 5.9 %shard_map.120 = bf16[8192,2048]{1,0:T(8,128)(2,1)} custom-call(s32[1]{0:T(128)} %bitcast.off, bf16[2048,2048]{1,0:T(8,128)(2,1)} %collective-permute-done.5.got, bf16[8192,2048]{1,0:T(8,128)(2,1)} %shard_map.119._), custom_call_target="tpu_custom_call", output_to_operand_aliasing={{}: (2, {})} | custom-call | flops 4194304 | bytes 16777216 | tf_op jit(solution)/shard_map/pallas_call | solution.py:432
  (2 shorter events, 0.0 us)
Async XLA Ops:
  223.9 31.7 %collective-permute-start = (f32[512,2048]{1,0:T(8,128)}, f32[512,2048]{1,0:T(8,128)}, u32[]{:S(2)}, u32[]{:S(2)}) collective-permute-start(f32[512,2048]{1,0:T(8,128)} %shard_map.112), channel_id=1, source_target_pairs={{0,1},{1,0},{2,3},{3,2},{4,5},{5,4},{6,7},{7,6}} | collective-permute-start | bytes 12582920 | tf_op jit(solution)/shard_map/ppermute | solution.py:471
  244.8 26.8 %collective-permute-start.2 = (f32[2048,512]{1,0:T(8,128)}, f32[2048,512]{1,0:T(8,128)}, u32[]{:S(2)}, u32[]{:S(2)}) collective-permute-start(f32[2048,512]{1,0:T(8,128)} %get-tuple-element.42), channel_id=1, source_target_pairs={{0,1},{1,0},{2,3},{3,2},{4,5},{5,4},{6,7},{7,6}} | collective-permute-start | bytes 12582920 | tf_op jit(solution)/shard_map/ppermute | solution.py:471
  246.2 7.6 %collective-permute-start.1 = (f32[2048,128]{1,0:T(8,128)S(1)}, f32[2048,128]{1,0:T(8,128)}, u32[]{:S(2)}, u32[]{:S(2)}) collective-permute-start(f32[2048,128]{1,0:T(8,128)S(1)} %constant_dynamic-slice_fusion.1), channel_id=1, source_target_pairs={{0,1},{1,0},{2,3},{3,2},{4,5},{5,4},{6,7},{7,6}} | collective-permute-start | bytes 3145736 | tf_op jit(solution)/shard_map/ppermute | solution.py:471
  344.1 38.4 %collective-permute-start.4 = (bf16[4096,2048]{1,0:T(8,128)(2,1)}, bf16[4096,2048]{1,0:T(8,128)(2,1)}, u32[]{:S(2)}, u32[]{:S(2)}) collective-permute-start(bf16[4096,2048]{1,0:T(8,128)(2,1)} %get-tuple-element.52), channel_id=1, source_target_pairs={{0,1},{1,0},{2,3},{3,2},{4,5},{5,4},{6,7},{7,6}} | collective-permute-start | bytes 50331656 | tf_op jit(solution)/shard_map/ppermute | solution.py:471
  344.2 14.2 %collective-permute-start.3 = (f32[1024,128]{1,0:T(8,128)S(1)}, f32[1024,128]{1,0:T(8,128)S(1)}, u32[]{:S(2)}, u32[]{:S(2)}) collective-permute-start(f32[1024,128]{1,0:T(8,128)S(1)} %constant_dynamic-slice_fusion), channel_id=1, source_target_pairs={{0,4},{4,0},{1,5},{5,1},{2,6},{6,2},{3,7},{7,3}} | collective-permute-start | bytes 1572872 | tf_op jit(solution)/shard_map/ppermute | solution.py:474
  382.6 125.7 %collective-permute-start.6 = (bf16[2048,2048]{1,0:T(8,128)(2,1)}, bf16[2048,2048]{1,0:T(8,128)(2,1)}, u32[]{:S(2)}, u32[]{:S(2)}) collective-permute-start(bf16[2048,2048]{1,0:T(8,128)(2,1)} %get-tuple-element.55), channel_id=1, source_target_pairs={{0,1},{1,0},{2,3},{3,2},{4,5},{5,4},{6,7},{7,6}} | collective-permute-start | bytes 25165832 | tf_op jit(solution)/shard_map/ppermute | solution.py:471
  415.0 107.2 %collective-permute-start.5 = (bf16[2048,2048]{1,0:T(8,128)(2,1)}, bf16[2048,2048]{1,0:T(8,128)(2,1)}, u32[]{:S(2)}, u32[]{:S(2)}) collective-permute-start(bf16[2048,2048]{1,0:T(8,128)(2,1)} %get-tuple-element.59), channel_id=1, source_target_pairs={{0,1},{1,0},{2,3},{3,2},{4,5},{5,4},{6,7},{7,6}} | collective-permute-start | bytes 25165832 | tf_op jit(solution)/shard_map/ppermute | solution.py:471
  415.5 48.8 %collective-permute-start.8 = (f32[1024,512]{1,0:T(8,128)}, f32[1024,512]{1,0:T(8,128)}, u32[]{:S(2)}, u32[]{:S(2)}) collective-permute-start(f32[1024,512]{1,0:T(8,128)} %get-tuple-element.47), channel_id=1, source_target_pairs={{0,4},{4,0},{1,5},{5,1},{2,6},{6,2},{3,7},{7,3}} | collective-permute-start | bytes 6291464 | tf_op jit(solution)/shard_map/ppermute | solution.py:474
  416.0 92.3 %collective-permute-start.7 = (f32[512,1024]{1,0:T(8,128)}, f32[512,1024]{1,0:T(8,128)}, u32[]{:S(2)}, u32[]{:S(2)}) collective-permute-start(f32[512,1024]{1,0:T(8,128)} %get-tuple-element.44), channel_id=1, source_target_pairs={{0,4},{4,0},{1,5},{5,1},{2,6},{6,2},{3,7},{7,3}} | collective-permute-start | bytes 6291464 | tf_op jit(solution)/shard_map/ppermute | solution.py:474
  417.5 11.3 %collective-permute-start.9 = (bf16[1024,128]{1,0:T(8,128)(2,1)S(1)}, bf16[1024,128]{1,0:T(8,128)(2,1)S(1)}, u32[]{:S(2)}, u32[]{:S(2)}) collective-permute-start(bf16[1024,128]{1,0:T(8,128)(2,1)S(1)} %add_convert_fusion.2), channel_id=1, source_target_pairs={{0,1},{1,0},{2,3},{3,2},{4,5},{5,4},{6,7},{7,6}} | collective-permute-start | bytes 786440 | tf_op jit(solution)/shard_map/ppermute | solution.py:471
